TPU v7x, 512 devices: a whole 4x8x8 slice. The times are simulated.
512 devices in a mesh: ka: 256 (over y, z_lo, x, core), ga: 2 (over z_hi).
Axes of the slice: x: 4, y: 8, z: 8 (z_hi: 2, z_lo: 4; z = z_hi * 4 + z_lo), core: 2. Of those that a mesh axis runs over, the one named last changes fastest.
Arguments:
- pair_density: bfloat16 [2048, 32, 12032], P('ka', None, 'ga'), may hold values from -6 to 6
- coulomb: float32 [12032], P('ga'), may hold values from 3e-05 to 0.003
Outputs:
- kernel: float32 [65536, 1280], P(('ka', 'ga'))
All inputs are finite; a program needn't handle non-finite values.
Results may differ from a plain program's by a relative error of at most 0.0013.
Values may be sent and summed in bfloat16 or wider, within the bound.
No kernel may reach another device: no remote copies, remote signals or barrier semaphores. Data moves between devices by JAX's collectives and lax.ppermute only.
A program may use at most 64 MiB of HBM per device.

v0:
```python
import jax
import jax.numpy as jnp
from jax import lax
from jax.sharding import PartitionSpec as P

STEPS = 2


def shifted(value, axis, steps):
    count = lax.axis_size(axis)
    pairs = [(source, (source + steps) % count) for source in range(count)]
    return lax.ppermute(value, axis, pairs)


def in_blocks(array, dim, count):
    lengths = array.shape
    tiles = array.reshape(*lengths[:dim], count, lengths[dim] // count, *lengths[dim + 1 :])
    return jnp.moveaxis(tiles, dim, 0)


def sum_at_owner(array, axis, dim):
    count = lax.axis_size(axis)
    tiles = lax.all_to_all(in_blocks(array, dim, count), axis, 0, 0, tiled=True)
    return jnp.sum(tiles, axis=0)


def product(left, right):
    return lax.dot_general(
        left, right, (((1,), (1,)), ((), ())), preferred_element_type=jnp.float32
    )


def shards(pair_density, coulomb):
    shard_points, pairs, local_waves = pair_density.shape
    width = shard_points * pairs
    own = pair_density.reshape(width, local_waves)
    weighted = (own.astype(jnp.float32) * coulomb[None, :]).astype(jnp.bfloat16)
    lower_blocks = [None] * (STEPS + 1)
    upper_blocks = [None] * (STEPS + 1)
    lower_blocks[0] = product(weighted, own)
    below = pair_density
    above = pair_density
    for step in range(1, STEPS + 1):
        below = shifted(below, "ka", 1)
        above = shifted(above, "ka", -1)
        lower_blocks[step] = product(weighted, below.reshape(width, local_waves))
        above_rows = above.reshape(width, local_waves)
        above_weighted = (above_rows.astype(jnp.float32) * coulomb[None, :]).astype(jnp.bfloat16)
        upper_blocks[step] = product(own, above_weighted)
    ordered = [lower_blocks[step] for step in range(STEPS, -1, -1)]
    joined_blocks = ordered + [upper_blocks[step] for step in range(1, STEPS + 1)]
    stacked = jnp.concatenate(joined_blocks, axis=1)
    summed = sum_at_owner(stacked, "ga", 0)
    return summed


def solution(mesh):
    in_specs = (P("ka", None, "ga"), P("ga"))
    out_specs = P(("ka", "ga"), None)
    return jax.shard_map(shards, mesh=mesh, in_specs=in_specs, out_specs=out_specs, check_vma=False)
```

profile of v0, /device:TPU:40, one launch (start us, length us, event | category | flops | bytes accessed | tf_op | source)
XLA Modules:
  0.0 137.9 jit_solution(6032954273371752020)
XLA Ops:
  0.0 10.3 %collective-permute-start.2 = (bf16[8,32,6016]{2,1,0:T(8,128)(2,1)}, bf16[8,32,6016]{2,1,0:T(8,128)(2,1)S(1)}, u32[]{:S(2)}, u32[]{:S(2)}) collective-permute-start(bf16[8,32,6016]{2,1,0:T(8,128)(2,1)} %param.2), channel_id=1, source_target_pairs={{0,510},{2,0},{4,2},{6,4},{8,6},{10,8},{12,10},{14,12},{16,14},{18... | collective-permute-start | bytes 9240584 | tf_op jit(solution)/shard_map/ppermute | solution.py:12
  10.3 1.9 %collective-permute-start = (bf16[8,32,6016]{2,1,0:T(8,128)(2,1)}, bf16[8,32,6016]{2,1,0:T(8,128)(2,1)}, u32[]{:S(2)}, u32[]{:S(2)}) collective-permute-start(bf16[8,32,6016]{2,1,0:T(8,128)(2,1)} %param.2), channel_id=1, source_target_pairs={{0,2},{2,4},{4,6},{6,8},{8,10},{10,12},{12,14},{14,16},{16,18},{18... | collective-permute-start | bytes 9240584 | tf_op jit(solution)/shard_map/ppermute | solution.py:12
  12.2 32.4 %collective-permute-done.2 = bf16[8,32,6016]{2,1,0:T(8,128)(2,1)S(1)} collective-permute-done((bf16[8,32,6016]{2,1,0:T(8,128)(2,1)}, bf16[8,32,6016]{2,1,0:T(8,128)(2,1)S(1)}, u32[]{:S(2)}, u32[]{:S(2)}) %collective-permute-start.2) | collective-permute-done | bytes 3080224 | tf_op jit(solution)/shard_map/ppermute | solution.py:12
  44.7 8.5 %collective-permute-start.3 = (bf16[8,32,6016]{2,1,0:T(8,128)(2,1)S(1)}, bf16[8,32,6016]{2,1,0:T(8,128)(2,1)S(1)}, u32[]{:S(2)}, u32[]{:S(2)}) collective-permute-start(bf16[8,32,6016]{2,1,0:T(8,128)(2,1)S(1)} %collective-permute-done.2), channel_id=1, source_target_pairs={{0,510},{2,0},{4,2},{6,4},{8,6},{10,8},{12,10},{14,12},{16,14},{18... | collective-permute-start | bytes 9240584 | tf_op jit(solution)/shard_map/ppermute | solution.py:12
  53.2 0.1 collective-permute-done
  53.3 1.9 %collective-permute-start.1 = (bf16[8,32,6016]{2,1,0:T(8,128)(2,1)}, bf16[8,32,6016]{2,1,0:T(8,128)(2,1)}, u32[]{:S(2)}, u32[]{:S(2)}) collective-permute-start(bf16[8,32,6016]{2,1,0:T(8,128)(2,1)} %collective-permute-done), channel_id=1, source_target_pairs={{0,2},{2,4},{4,6},{6,8},{8,10},{10,12},{12,14},{14,16},{16,18},{18... | collective-permute-start | bytes 9240584 | tf_op jit(solution)/shard_map/ppermute | solution.py:12
  55.2 32.0 %collective-permute-done.3 = bf16[8,32,6016]{2,1,0:T(8,128)(2,1)S(1)} collective-permute-done((bf16[8,32,6016]{2,1,0:T(8,128)(2,1)S(1)}, bf16[8,32,6016]{2,1,0:T(8,128)(2,1)S(1)}, u32[]{:S(2)}, u32[]{:S(2)}) %collective-permute-start.3) | collective-permute-done | bytes 3080224 | tf_op jit(solution)/shard_map/ppermute | solution.py:12
  87.3 5.3 %multiply_convert_fusion = (bf16[8,32,6016]{2,1,0:T(8,128)(2,1)S(1)}, bf16[8,32,6016]{2,1,0:T(8,128)(2,1)S(1)}, bf16[8,32,6016]{2,1,0:T(8,128)(2,1)}) fusion(bf16[8,32,6016]{2,1,0:T(8,128)(2,1)S(1)} %collective-permute-done.3, f32[6016]{0:T(1024)} %param.3, bf16[8,32,6016]{2,1,0:T(8,128)(2,1)S(1)} %collective-permute-done.2, bf16[8,32,6016]{2,1,0:T(8,128)(2,1)} %param.2), kind=kLoop, calls=%fused_computation | loop fusion | flops 13860864 | bytes 18505216 | tf_op jit(solution)/shard_map/convert_element_type | solution.py:48
  92.5 3.8 %collective-permute-done.1 = bf16[8,32,6016]{2,1,0:T(8,128)(2,1)} collective-permute-done((bf16[8,32,6016]{2,1,0:T(8,128)(2,1)}, bf16[8,32,6016]{2,1,0:T(8,128)(2,1)}, u32[]{:S(2)}, u32[]{:S(2)}) %collective-permute-start.1) | collective-permute-done | bytes 3080224 | tf_op jit(solution)/shard_map/ppermute | solution.py:12
  96.3 0.0 copy-start.1
  96.3 4.0 %convolution_dynamic-update-slice_fusion.2 = f32[256,1280]{0,1:T(8,128)S(1)} fusion(bf16[256,6016]{1,0:T(8,128)(2,1)} %bitcast.34, bf16[256,6016]{1,0:T(8,128)(2,1)} %bitcast.1), kind=kOutput, calls=%fused_computation.6 | convolution fusion | flops 788529152 | bytes 6422528 | tf_op jit(solution)/shard_map/dot_general | solution.py:28
  100.3 0.0 copy-done.1
  100.3 0.0 copy-start
  100.3 3.0 %convolution_dynamic-update-slice_fusion.1 = f32[256,1280]{0,1:T(8,128)S(1)} fusion(f32[256,1280]{0,1:T(8,128)S(1)} %convolution_dynamic-update-slice_fusion.2, bf16[256,6016]{1,0:T(8,128)(2,1)S(1)} %bitcast.35, bf16[256,6016]{1,0:T(8,128)(2,1)} %bitcast.2), kind=kOutput, calls=%fused_computation.5 | convolution fusion | flops 788529152 | bytes 6422528 | tf_op jit(solution)/shard_map/dot_general | solution.py:28
  103.4 0.0 copy-done
  103.4 1.0 convolution_dynamic-update-slice_fusion
  104.4 1.0 fusion.1
  105.4 1.0 fusion
  106.4 0.1 copy_bitcast_fusion
  106.5 30.2 %all_to_all.5 = f32[2,128,1280]{1,2,0:T(8,128)S(1)} all-to-all(f32[2,128,1280]{1,2,0:T(8,128)S(1)} %copy_bitcast_fusion), channel_id=1, replica_groups=mesh['ka'=256,'ga'=2] {'ga'}, dimensions={0} | all-to-all | bytes 2621440 | tf_op jit(solution)/shard_map/all_to_all | solution.py:23
  136.7 0.1 reduce_sum.9
  136.9 1.1 copy.5
Async XLA Ops:
  0.0 44.7 %collective-permute-start.2 = (bf16[8,32,6016]{2,1,0:T(8,128)(2,1)}, bf16[8,32,6016]{2,1,0:T(8,128)(2,1)S(1)}, u32[]{:S(2)}, u32[]{:S(2)}) collective-permute-start(bf16[8,32,6016]{2,1,0:T(8,128)(2,1)} %param.2), channel_id=1, source_target_pairs={{0,510},{2,0},{4,2},{6,4},{8,6},{10,8},{12,10},{14,12},{16,14},{18... | collective-permute-start | bytes 9240584 | tf_op jit(solution)/shard_map/ppermute | solution.py:12
  10.3 43.0 %collective-permute-start = (bf16[8,32,6016]{2,1,0:T(8,128)(2,1)}, bf16[8,32,6016]{2,1,0:T(8,128)(2,1)}, u32[]{:S(2)}, u32[]{:S(2)}) collective-permute-start(bf16[8,32,6016]{2,1,0:T(8,128)(2,1)} %param.2), channel_id=1, source_target_pairs={{0,2},{2,4},{4,6},{6,8},{8,10},{10,12},{12,14},{14,16},{16,18},{18... | collective-permute-start | bytes 9240584 | tf_op jit(solution)/shard_map/ppermute | solution.py:12
  44.7 42.6 %collective-permute-start.3 = (bf16[8,32,6016]{2,1,0:T(8,128)(2,1)S(1)}, bf16[8,32,6016]{2,1,0:T(8,128)(2,1)S(1)}, u32[]{:S(2)}, u32[]{:S(2)}) collective-permute-start(bf16[8,32,6016]{2,1,0:T(8,128)(2,1)S(1)} %collective-permute-done.2), channel_id=1, source_target_pairs={{0,510},{2,0},{4,2},{6,4},{8,6},{10,8},{12,10},{14,12},{16,14},{18... | collective-permute-start | bytes 9240584 | tf_op jit(solution)/shard_map/ppermute | solution.py:12
  53.3 43.0 %collective-permute-start.1 = (bf16[8,32,6016]{2,1,0:T(8,128)(2,1)}, bf16[8,32,6016]{2,1,0:T(8,128)(2,1)}, u32[]{:S(2)}, u32[]{:S(2)}) collective-permute-start(bf16[8,32,6016]{2,1,0:T(8,128)(2,1)} %collective-permute-done), channel_id=1, source_target_pairs={{0,2},{2,4},{4,6},{6,8},{8,10},{10,12},{12,14},{14,16},{16,18},{18... | collective-permute-start | bytes 9240584 | tf_op jit(solution)/shard_map/ppermute | solution.py:12
  96.3 4.0 %copy-start.1 = (bf16[8,32,6016]{2,1,0:T(8,128)(2,1)S(1)}, bf16[8,32,6016]{2,1,0:T(8,128)(2,1)}, u32[]{:S(2)}) copy-start(bf16[8,32,6016]{2,1,0:T(8,128)(2,1)} %get-tuple-element.7) | copy-start | bytes 9240580
  100.3 3.1 %copy-start = (bf16[8,32,6016]{2,1,0:T(8,128)(2,1)S(1)}, bf16[8,32,6016]{2,1,0:T(8,128)(2,1)}, u32[]{:S(2)}) copy-start(bf16[8,32,6016]{2,1,0:T(8,128)(2,1)} %param.2) | copy-start | bytes 9240580
where the time goes:
time: 138 us
  waiting for transfers between devices  68.4 us (50%)
  blocking collectives  30.2 us (22%)
  starting transfers between devices  22.6 us (16%)
  matrix products  10 us (7%)
  other arithmetic  5.39 us (4%)
    ppermute x4, waiting for transfers between devices, shifted(): return lax.ppermute(value, axis, pairs)  68.4 us
    all_to_all x1, blocking collectives, sum_at_owner(): tiles = lax.all_to_all(in_blocks(array, dim, count), axis, 0, 0, tiled=True)  30.2 us
    ppermute x4, starting transfers between devices, shifted(): return lax.ppermute(value, axis, pairs)  22.6 us
    dot_general x5, matrix products, product(): lax.dot_general(left, right, (((1,), (1,)), ((), ())), preferred_element_...  10 us
    convert_element_type x1, other arithmetic, shards(): (above_rows.astype(jnp.float32) * coulomb[None, :]).astype(jnp.bfloat16)  5.25 us
  transfers between devices with their start and end apart: 4, of which 4 were waited for; matrix products, arithmetic and copies ran while one was open for 4% of the time, Pallas kernels for 0%

commit v1 on v0

v1 whole, which is shorter than its diff:
```python
import jax
import jax.numpy as jnp
from jax import lax
from jax.experimental import pallas as pl
from jax.experimental.pallas import tpu as pltpu
from jax.sharding import PartitionSpec as P

ROWS = 256
HALF = 128
EXTRA = 8
PEAK = 14.0

F32 = jnp.float32
BF16 = jnp.bfloat16
F16 = jnp.float16


def nt_dot(left, right):
    return lax.dot_general(left, right, (((1,), (1,)), ((), ())), preferred_element_type=F32)


def scale_rows(source, target, at, factor):
    def body(step, _):
        rows = pl.multiple_of(step * 16, 16)
        piece = source[pl.ds(rows, 16), :].astype(F32) * factor
        target[pl.ds(at + rows, 16), :] = piece.astype(BF16)
        return 0

    lax.fori_loop(0, ROWS // 16, body, 0)


def exponent_for(biggest):
    return PEAK - jnp.ceil(jnp.log2(jnp.maximum(biggest, 1e-30)))


def pack(message, block, exponent, columns):
    message[0:HALF, columns] = block * jnp.exp2(exponent)
    message[HALF : HALF + EXTRA, columns] = jnp.broadcast_to(exponent, (EXTRA, ROWS))


def unpack(message, columns):
    exponent = message[HALF : HALF + EXTRA, columns][0:1, :]
    return message[0:HALF, columns] * jnp.exp2(-exponent)


def sides(where_ref, coulomb_ref):
    even = where_ref[0] == 0
    weights = coulomb_ref[...]
    ones = jnp.ones_like(weights)
    return jnp.where(even, ones, weights), jnp.where(even, weights, ones)


def early_kernel(where_ref, coulomb_ref, own, sib, keep, message, left, weighted, acc):
    left_factor, right_factor = sides(where_ref, coulomb_ref)
    half = where_ref[1]
    mine = pl.multiple_of(half * HALF, HALF)
    other = pl.multiple_of((1 - half) * HALF, HALF)
    scale_rows(own, left, 0, left_factor)
    scale_rows(sib, left, ROWS, left_factor)
    scale_rows(own, weighted, 0, coulomb_ref[...])
    acc[:, 0:ROWS] = nt_dot(weighted[...], own[...])
    scale_rows(sib, weighted, 0, right_factor)
    acc[:, ROWS : 2 * ROWS] = nt_dot(left[0:ROWS, :], weighted[...])
    biggest = jnp.max(jnp.abs(acc[...]), axis=(0, 1), keepdims=True)
    exponent = exponent_for(biggest)
    keep[...] = acc[pl.ds(mine, HALF), :]
    for at in range(2):
        columns = slice(at * ROWS, (at + 1) * ROWS)
        pack(message, acc[pl.ds(other, HALF), columns], exponent, columns)


def late_kernel(where_ref, coulomb_ref, far, left, keep, to_sib, to_far, over, sib_over, far_over, weighted, acc, turned):
    _, right_factor = sides(where_ref, coulomb_ref)
    half = where_ref[1]
    mine = pl.multiple_of(half * HALF, HALF)
    other = pl.multiple_of((1 - half) * HALF, HALF)
    scale_rows(far, weighted, 0, right_factor)
    acc[...] = nt_dot(left[...], weighted[...])
    biggest = jnp.max(jnp.abs(acc[...]), axis=(0, 1), keepdims=True)
    exponent = exponent_for(biggest)
    turned[...] = acc[0:ROWS, :].T
    columns = slice(0, ROWS)
    keep[...] = acc[pl.ds(mine, HALF), :]
    pack(over, acc[pl.ds(other, HALF), :], exponent, columns)
    to_sib[...] = acc[pl.ds(ROWS + mine, HALF), :]
    pack(sib_over, acc[pl.ds(ROWS + other, HALF), :], exponent, columns)
    to_far[...] = turned[pl.ds(mine, HALF), :]
    pack(far_over, turned[pl.ds(other, HALF), :], exponent, columns)


def final_kernel(where_ref, early, early_over, keep, over, from_sib, sib_over, from_far, far_over, out):
    columns = slice(0, ROWS)
    nearest = early[:, 0:ROWS] + unpack(early_over, slice(0, ROWS))
    inside = early[:, ROWS : 2 * ROWS] + unpack(early_over, slice(ROWS, 2 * ROWS))
    outside = keep[...] + unpack(over, columns)
    beside = from_sib[...] + unpack(sib_over, columns)
    returned = from_far[...] + unpack(far_over, columns)
    order = [returned, beside, nearest, inside, outside]

    @pl.when(where_ref[0] == 0)
    def _():
        for at, block in enumerate(order):
            out[:, at * ROWS : (at + 1) * ROWS] = block

    @pl.when(where_ref[0] != 0)
    def _():
        for at, block in enumerate(reversed(order)):
            out[:, at * ROWS : (at + 1) * ROWS] = block


def vmem():
    return pl.BlockSpec(memory_space=pltpu.VMEM)


def smem():
    return pl.BlockSpec(memory_space=pltpu.SMEM)


def call(kernel, name, inputs, outputs, scratch):
    return pl.pallas_call(
        kernel,
        name=name,
        in_specs=[smem()] + [vmem()] * (inputs - 1),
        out_specs=[vmem()] * len(outputs),
        out_shape=[jax.ShapeDtypeStruct(shape, kind) for shape, kind in outputs],
        scratch_shapes=[pltpu.VMEM(shape, kind) for shape, kind in scratch],
        compiler_params=pltpu.CompilerParams(vmem_limit_bytes=56 * 1024 * 1024),
    )


def over_ga(value, pairs):
    count = lax.axis_size("ga")
    moves = [(s * count + h, t * count + 1 - h) for s, t in pairs for h in range(count)]
    return lax.ppermute(value.astype(F16), ("ka", "ga"), moves).astype(F32)


def shards(pair_density, coulomb):
    shard_points, pairs, waves = pair_density.shape
    width = shard_points * pairs
    count = lax.axis_size("ka")
    index = lax.axis_index("ka")
    half = lax.axis_index("ga")
    where = jnp.stack([index % 2, half]).astype(jnp.int32)
    same = [(i, i) for i in range(count)]
    swap = [(i, i ^ 1) for i in range(count)]
    send = [(i, (i - 2) % count if i % 2 == 0 else (i + 2) % count) for i in range(count)]
    back = [(t, s) for s, t in send]
    factor = coulomb.reshape(1, waves)

    far = lax.ppermute(pair_density, "ka", send).reshape(width, waves)
    sib = lax.ppermute(pair_density, "ka", swap).reshape(width, waves)
    own = pair_density.reshape(width, waves)
    early, early_msg, left = call(
        early_kernel,
        "early",
        4,
        [((HALF, 2 * ROWS), F32), ((HALF + EXTRA, 2 * ROWS), F32), ((2 * ROWS, waves), BF16)],
        [((ROWS, waves), BF16), ((ROWS, 2 * ROWS), F32)],
    )(where, factor, own, sib)
    early_over = over_ga(early_msg, same)
    keep, to_sib, to_far, over, sib_over, far_over = call(
        late_kernel,
        "late",
        4,
        [((HALF, ROWS), F32)] * 3 + [((HALF + EXTRA, ROWS), F32)] * 3,
        [((ROWS, waves), BF16), ((2 * ROWS, ROWS), F32), ((ROWS, ROWS), F32)],
    )(where, factor, far, left)
    far_over = over_ga(far_over, back)
    sib_over = over_ga(sib_over, swap)
    over = over_ga(over, same)
    from_far = lax.ppermute(to_far, "ka", back)
    from_sib = lax.ppermute(to_sib, "ka", swap)
    (out,) = call(final_kernel, "final", 9, [((HALF, 5 * ROWS), F32)], [])(
        where, early, early_over, keep, over, from_sib, sib_over, from_far, far_over
    )
    return out


def solution(mesh):
    in_specs = (P("ka", None, "ga"), P("ga"))
    out_specs = P(("ka", "ga"), None)
    return jax.shard_map(shards, mesh=mesh, in_specs=in_specs, out_specs=out_specs, check_vma=False)
```

time: 138 us -> 103 us (0.75)
  the two profiles are of different devices: /device:TPU:40 before, /device:TPU:32 now
where the time goes in v1:
time: 103 us
  starting transfers between devices  43.9 us (43%)
  waiting for transfers between devices  27.2 us (26%)
  Pallas kernels  21.5 us (21%)
  other arithmetic  6.19 us (6%)
  local copies, waits for them, and re-layouts  3.65 us (4%)
    ppermute x4, starting transfers between devices, over_ga(): return lax.ppermute(value.astype(F16), ('ka', 'ga'), moves).astype(F32)  26 us
    ppermute x1, waiting for transfers between devices, shards(): far = lax.ppermute(pair_density, 'ka', send).reshape(width, waves)  18.8 us
    pallas_call x1, Pallas kernels, shards(): call(early_kernel, 'early', 4, [((HALF, 2 * ROWS), F32), ((HALF + EXTRA,...  12 us
    ppermute x1, starting transfers between devices, shards(): far = lax.ppermute(pair_density, 'ka', send).reshape(width, waves)  9.98 us
    ppermute x4, waiting for transfers between devices, over_ga(): return lax.ppermute(value.astype(F16), ('ka', 'ga'), moves).astype(F32)  8.38 us
    pallas_call x1, Pallas kernels, shards(): call(late_kernel, 'late', 4, [((HALF, ROWS), F32)] * 3 + [((HALF + EXTRA,...  7.21 us
    convert_element_type x8, other arithmetic, over_ga(): return lax.ppermute(value.astype(F16), ('ka', 'ga'), moves).astype(F32)  5.52 us
    ppermute x1, starting transfers between devices, shards(): from_sib = lax.ppermute(to_sib, 'ka', swap)  4.1 us
  transfers between devices with their start and end apart: 8, of which 2 were waited for; matrix products, arithmetic and copies ran while one was open for 6% of the time, Pallas kernels for 12%

profile of v1, /device:TPU:32, one launch (start us, length us, event | category | flops | bytes accessed | tf_op | source)
XLA Modules:
  0.0 102.5 jit_solution(11376884797392356933)
XLA Ops:
  0.0 1.9 %collective-permute-start = (bf16[8,32,6016]{2,1,0:T(8,128)(2,1)}, bf16[8,32,6016]{2,1,0:T(8,128)(2,1)S(1)}, u32[]{:S(2)}, u32[]{:S(2)}) collective-permute-start(bf16[8,32,6016]{2,1,0:T(8,128)(2,1)} %param.2), channel_id=1, source_target_pairs={{0,2},{2,0},{4,6},{6,4},{8,10},{10,8},{12,14},{14,12},{16,18},{18,... | collective-permute-start | bytes 9240584 | tf_op jit(solution)/shard_map/ppermute | solution.py:151
  1.9 10.0 %collective-permute-start.2 = (bf16[8,32,6016]{2,1,0:T(8,128)(2,1)}, bf16[8,32,6016]{2,1,0:T(8,128)(2,1)}, u32[]{:S(2)}, u32[]{:S(2)}) collective-permute-start(bf16[8,32,6016]{2,1,0:T(8,128)(2,1)} %param.2), channel_id=1, source_target_pairs={{0,508},{2,6},{4,0},{6,10},{8,4},{10,14},{12,8},{14,18},{16,12},{1... | collective-permute-start | bytes 9240584 | tf_op jit(solution)/shard_map/ppermute | solution.py:150
  11.9 1.4 %reshape.12.coulomb_ref = f32[1,6016]{1,0:T(1,128)} reshape(f32[6016]{0:T(1024)} %param.3) | data formatting | bytes 48128 | tf_op jit(solution)/shard_map/reshape | solution.py:148
  13.3 0.7 pad_add_fusion.where_ref
  13.9 0.0 collective-permute-done
  13.9 1.6 %copy-done = bf16[8,32,6016]{2,1,0:T(8,128)(2,1)} copy-done((bf16[8,32,6016]{2,1,0:T(8,128)(2,1)}, bf16[8,32,6016]{2,1,0:T(8,128)(2,1)S(1)}, u32[]{:S(2)}) %copy-start) | copy-done | bytes 3080216
  15.6 12.0 %early.1 = (f32[128,512]{1,0:T(8,128)}, f32[136,512]{1,0:T(8,128)}, bf16[512,6016]{1,0:T(8,128)(2,1)}) custom-call(s32[2]{0:T(128)} %pad_add_fusion.where_ref, f32[1,6016]{1,0:T(1,128)} %reshape.12.coulomb_ref, bf16[256,6016]{1,0:T(8,128)(2,1)} %bitcast.5, bf16[256,6016]{1,0:T(8,128)(2,1)} %bitcast.6), custom_call_target="tpu_custom_call" | custom-call | tf_op jit(solution)/shard_map/early/pallas_call | solution.py:153
  27.5 18.8 %collective-permute-done.2 = bf16[8,32,6016]{2,1,0:T(8,128)(2,1)} collective-permute-done((bf16[8,32,6016]{2,1,0:T(8,128)(2,1)}, bf16[8,32,6016]{2,1,0:T(8,128)(2,1)}, u32[]{:S(2)}, u32[]{:S(2)}) %collective-permute-start.2) | collective-permute-done | bytes 3080224 | tf_op jit(solution)/shard_map/ppermute | solution.py:150
  46.3 7.2 %late.1 = (f32[128,256]{1,0:T(8,128)}, f32[128,256]{1,0:T(8,128)}, f32[128,256]{1,0:T(8,128)}, f32[136,256]{1,0:T(8,128)}, f32[136,256]{1,0:T(8,128)}, /*index=5*/f32[136,256]{1,0:T(8,128)}) custom-call(s32[2]{0:T(128)} %pad_add_fusion.where_ref, f32[1,6016]{1,0:T(1,128)} %reshape.12.coulomb_ref, bf16[256,6016]{1,0:T(8,128)(2,1)} %bitcast.4.far, ...), custom_call_target="tpu_custom_call" | custom-call | tf_op jit(solution)/shard_map/late/pallas_call | solution.py:161
  53.5 0.9 convert_element_type.26
  54.4 8.2 %collective-permute-start.3 = (f16[136,256]{1,0:T(8,128)(2,1)S(1)}, f16[136,256]{1,0:T(8,128)(2,1)S(1)}, u32[]{:S(2)}, u32[]{:S(2)}) collective-permute-start(f16[136,256]{1,0:T(8,128)(2,1)S(1)} %convert_element_type.26), channel_id=1, source_target_pairs={{0,1},{1,0},{2,3},{3,2},{4,5},{5,4},{6,7},{7,6},{8,9},{9,8},{10,11... | collective-permute-start | bytes 208904 | tf_op jit(solution)/shard_map/ppermute | solution.py:134
  62.6 0.0 copy-done.1
  62.7 1.9 %collective-permute-start.1 = (f16[136,512]{1,0:T(8,128)(2,1)S(1)}, f16[136,512]{1,0:T(8,128)(2,1)S(1)}, u32[]{:S(2)}, u32[]{:S(2)}) collective-permute-start(f16[136,512]{1,0:T(8,128)(2,1)S(1)} %convert_element_type.24), channel_id=1, source_target_pairs={{0,1},{1,0},{2,3},{3,2},{4,5},{5,4},{6,7},{7,6},{8,9},{9,8},{10,11... | collective-permute-start | bytes 417800 | tf_op jit(solution)/shard_map/ppermute | solution.py:134
  64.6 4.1 %collective-permute-start.4 = (f32[128,256]{1,0:T(8,128)}, f32[128,256]{1,0:T(8,128)S(1)}, u32[]{:S(2)}, u32[]{:S(2)}) collective-permute-start(f32[128,256]{1,0:T(8,128)} %get-tuple-element.19), channel_id=1, source_target_pairs={{0,2},{2,0},{4,6},{6,4},{8,10},{10,8},{12,14},{14,12},{16,18},{18,... | collective-permute-start | bytes 393224 | tf_op jit(solution)/shard_map/ppermute | solution.py:172
  68.7 1.9 %collective-permute-start.6 = (f32[128,256]{1,0:T(8,128)}, f32[128,256]{1,0:T(8,128)S(1)}, u32[]{:S(2)}, u32[]{:S(2)}) collective-permute-start(f32[128,256]{1,0:T(8,128)} %get-tuple-element.21), channel_id=1, source_target_pairs={{508,0},{6,2},{0,4},{10,6},{4,8},{14,10},{8,12},{18,14},{12,16},{2... | collective-permute-start | bytes 393224 | tf_op jit(solution)/shard_map/ppermute | solution.py:171
  70.7 0.9 convert_element_type.28
  71.6 14.0 %collective-permute-start.5 = (f16[136,256]{1,0:T(8,128)(2,1)S(1)}, f16[136,256]{1,0:T(8,128)(2,1)S(1)}, u32[]{:S(2)}, u32[]{:S(2)}) collective-permute-start(f16[136,256]{1,0:T(8,128)(2,1)S(1)} %convert_element_type.28), channel_id=1, source_target_pairs={{0,3},{1,2},{2,1},{3,0},{4,7},{5,6},{6,5},{7,4},{8,11},{9,10},{10,... | collective-permute-start | bytes 208904 | tf_op jit(solution)/shard_map/ppermute | solution.py:134
  85.5 0.9 convert_element_type.30
  86.5 0.0 collective-permute-done.3
  86.5 1.9 %collective-permute-start.7 = (f16[136,256]{1,0:T(8,128)(2,1)S(1)}, f16[136,256]{1,0:T(8,128)(2,1)S(1)}, u32[]{:S(2)}, u32[]{:S(2)}) collective-permute-start(f16[136,256]{1,0:T(8,128)(2,1)S(1)} %convert_element_type.30), channel_id=1, source_target_pairs={{508,1},{509,0},{6,3},{7,2},{0,5},{1,4},{10,7},{11,6},{4,9},{5,8},... | collective-permute-start | bytes 208904 | tf_op jit(solution)/shard_map/ppermute | solution.py:134
  88.4 0.7 convert_element_type.27.over
  89.1 0.0 collective-permute-done.5
  89.1 0.7 convert_element_type.29.sib_over
  89.7 8.4 %collective-permute-done.7 = f16[136,256]{1,0:T(8,128)(2,1)S(1)} collective-permute-done((f16[136,256]{1,0:T(8,128)(2,1)S(1)}, f16[136,256]{1,0:T(8,128)(2,1)S(1)}, u32[]{:S(2)}, u32[]{:S(2)}) %collective-permute-start.7) | collective-permute-done | bytes 69664 | tf_op jit(solution)/shard_map/ppermute | solution.py:134
  98.1 0.7 convert_element_type.31.far_over
  98.8 0.0 collective-permute-done.1
  98.8 0.7 convert_element_type.25.early_over
  99.5 0.0 collective-permute-done.4.from_sib
  99.5 0.0 collective-permute-done.6.from_far
  99.5 0.6 copy-done.2
  100.2 0.1 copy-done.3
  100.2 2.3 %final.1 = f32[128,1280]{1,0:T(8,128)} custom-call(s32[2]{0:T(128)} %pad_add_fusion.where_ref, f32[128,512]{1,0:T(8,128)} %get-tuple-element.14.early, f32[136,512]{1,0:T(8,128)} %convert_element_type.25.early_over, f32[128,256]{1,0:T(8,128)} %get-tuple-element.17.keep, f32[136,256]{1,0:T(8,128)} %convert_element_type.27.over, f32[128,256]{1,0:T(8,128)} %copy-done.2, ...), custom_call_target="tpu_custom_call" | custom-call | tf_op jit(solution)/shard_map/final/pallas_call | solution.py:173
  (5 shorter events, 0.0 us)
Async XLA Ops:
  0.0 13.9 %collective-permute-start = (bf16[8,32,6016]{2,1,0:T(8,128)(2,1)}, bf16[8,32,6016]{2,1,0:T(8,128)(2,1)S(1)}, u32[]{:S(2)}, u32[]{:S(2)}) collective-permute-start(bf16[8,32,6016]{2,1,0:T(8,128)(2,1)} %param.2), channel_id=1, source_target_pairs={{0,2},{2,0},{4,6},{6,4},{8,10},{10,8},{12,14},{14,12},{16,18},{18,... | collective-permute-start | bytes 9240584 | tf_op jit(solution)/shard_map/ppermute | solution.py:151
  1.9 44.4 %collective-permute-start.2 = (bf16[8,32,6016]{2,1,0:T(8,128)(2,1)}, bf16[8,32,6016]{2,1,0:T(8,128)(2,1)}, u32[]{:S(2)}, u32[]{:S(2)}) collective-permute-start(bf16[8,32,6016]{2,1,0:T(8,128)(2,1)} %param.2), channel_id=1, source_target_pairs={{0,508},{2,6},{4,0},{6,10},{8,4},{10,14},{12,8},{14,18},{16,12},{1... | collective-permute-start | bytes 9240584 | tf_op jit(solution)/shard_map/ppermute | solution.py:150
  13.9 1.6 %copy-start = (bf16[8,32,6016]{2,1,0:T(8,128)(2,1)}, bf16[8,32,6016]{2,1,0:T(8,128)(2,1)S(1)}, u32[]{:S(2)}) copy-start(bf16[8,32,6016]{2,1,0:T(8,128)(2,1)S(1)} %collective-permute-done) | copy-start | bytes 9240580
  46.3 16.4 %copy-start.1 = (f32[136,512]{1,0:T(8,128)S(1)}, f32[136,512]{1,0:T(8,128)}, u32[]{:S(2)}) copy-start(f32[136,512]{1,0:T(8,128)} %get-tuple-element.15) | copy-start | bytes 835588
  54.4 32.0 %collective-permute-start.3 = (f16[136,256]{1,0:T(8,128)(2,1)S(1)}, f16[136,256]{1,0:T(8,128)(2,1)S(1)}, u32[]{:S(2)}, u32[]{:S(2)}) collective-permute-start(f16[136,256]{1,0:T(8,128)(2,1)S(1)} %convert_element_type.26), channel_id=1, source_target_pairs={{0,1},{1,0},{2,3},{3,2},{4,5},{5,4},{6,7},{7,6},{8,9},{9,8},{10,11... | collective-permute-start | bytes 208904 | tf_op jit(solution)/shard_map/ppermute | solution.py:134
  62.7 36.1 %collective-permute-start.1 = (f16[136,512]{1,0:T(8,128)(2,1)S(1)}, f16[136,512]{1,0:T(8,128)(2,1)S(1)}, u32[]{:S(2)}, u32[]{:S(2)}) collective-permute-start(f16[136,512]{1,0:T(8,128)(2,1)S(1)} %convert_element_type.24), channel_id=1, source_target_pairs={{0,1},{1,0},{2,3},{3,2},{4,5},{5,4},{6,7},{7,6},{8,9},{9,8},{10,11... | collective-permute-start | bytes 417800 | tf_op jit(solution)/shard_map/ppermute | solution.py:134
  64.6 34.9 %collective-permute-start.4 = (f32[128,256]{1,0:T(8,128)}, f32[128,256]{1,0:T(8,128)S(1)}, u32[]{:S(2)}, u32[]{:S(2)}) collective-permute-start(f32[128,256]{1,0:T(8,128)} %get-tuple-element.19), channel_id=1, source_target_pairs={{0,2},{2,0},{4,6},{6,4},{8,10},{10,8},{12,14},{14,12},{16,18},{18,... | collective-permute-start | bytes 393224 | tf_op jit(solution)/shard_map/ppermute | solution.py:172
  68.7 30.8 %collective-permute-start.6 = (f32[128,256]{1,0:T(8,128)}, f32[128,256]{1,0:T(8,128)S(1)}, u32[]{:S(2)}, u32[]{:S(2)}) collective-permute-start(f32[128,256]{1,0:T(8,128)} %get-tuple-element.21), channel_id=1, source_target_pairs={{508,0},{6,2},{0,4},{10,6},{4,8},{14,10},{8,12},{18,14},{12,16},{2... | collective-permute-start | bytes 393224 | tf_op jit(solution)/shard_map/ppermute | solution.py:171
  71.6 17.5 %collective-permute-start.5 = (f16[136,256]{1,0:T(8,128)(2,1)S(1)}, f16[136,256]{1,0:T(8,128)(2,1)S(1)}, u32[]{:S(2)}, u32[]{:S(2)}) collective-permute-start(f16[136,256]{1,0:T(8,128)(2,1)S(1)} %convert_element_type.28), channel_id=1, source_target_pairs={{0,3},{1,2},{2,1},{3,0},{4,7},{5,6},{6,5},{7,4},{8,11},{9,10},{10,... | collective-permute-start | bytes 208904 | tf_op jit(solution)/shard_map/ppermute | solution.py:134
  86.5 11.6 %collective-permute-start.7 = (f16[136,256]{1,0:T(8,128)(2,1)S(1)}, f16[136,256]{1,0:T(8,128)(2,1)S(1)}, u32[]{:S(2)}, u32[]{:S(2)}) collective-permute-start(f16[136,256]{1,0:T(8,128)(2,1)S(1)} %convert_element_type.30), channel_id=1, source_target_pairs={{508,1},{509,0},{6,3},{7,2},{0,5},{1,4},{10,7},{11,6},{4,9},{5,8},... | collective-permute-start | bytes 208904 | tf_op jit(solution)/shard_map/ppermute | solution.py:134
  99.5 0.7 copy-start.2
  99.5 0.7 copy-start.3

commit v2 on v0

v2 whole, which is shorter than its diff:
```python
import jax
import jax.numpy as jnp
from jax import lax
from jax.experimental import pallas as pl
from jax.experimental.pallas import tpu as pltpu
from jax.sharding import PartitionSpec as P


ROWS = 256
HALF = 128
EXTRA = 8
PEAK = 14.0
STEP = 512

F32 = jnp.float32
BF16 = jnp.bfloat16
F16 = jnp.float16


def nt_dot(left, right):
    return lax.dot_general(left, right, (((1,), (1,)), ((), ())), preferred_element_type=F32)


def column_steps(waves):
    return [slice(at, min(at + STEP, waves)) for at in range(0, waves, STEP)]


def scaled(piece, factor):
    return (piece.astype(F32) * factor).astype(BF16)


def position():
    return lax.axis_index("ka") % 2 == 0, lax.axis_index("ga")


def exponent_for(biggest):
    return PEAK - jnp.ceil(jnp.log2(jnp.maximum(biggest, 1e-30)))


def send_exponent(message, exponent):
    message[HALF : HALF + EXTRA, :] = jnp.broadcast_to(exponent, (EXTRA, message.shape[1]))


def received(message, columns):
    return message[0:HALF, columns] * jnp.exp2(-message[HALF : HALF + 1, columns])


def early_kernel(coulomb, own, sib, keep, message, left):
    even, half = position()
    own_acc = jnp.zeros((ROWS, ROWS), F32)
    sib_acc = jnp.zeros((ROWS, ROWS), F32)
    for columns in column_steps(own.shape[1]):
        weight = coulomb[:, columns]
        ones = jnp.ones_like(weight)
        near = jnp.where(even, ones, weight)
        away = jnp.where(even, weight, ones)
        mine = own[:, columns]
        other = sib[:, columns]
        other_away = scaled(other, away)
        own_acc += nt_dot(scaled(mine, weight), mine)
        sib_acc += nt_dot(scaled(mine, near), other_away)
        left[0:ROWS, columns] = scaled(mine, away)
        left[ROWS : 2 * ROWS, columns] = other_away
    biggest = jnp.maximum(jnp.max(jnp.abs(own_acc)), jnp.max(jnp.abs(sib_acc)))
    exponent = exponent_for(jnp.full((1, 1), biggest))
    factor = jnp.exp2(exponent)
    send_exponent(message, exponent)
    for at, acc in ((0, own_acc), (ROWS, sib_acc)):
        columns = slice(at, at + ROWS)
        top, bottom = acc[0:HALF, :], acc[HALF:ROWS, :]
        keep[:, columns] = jnp.where(half == 0, top, bottom)
        message[0:HALF, columns] = jnp.where(half == 0, bottom, top) * factor


def late_kernel(coulomb, far, left, keep, across, corner, message):
    even, half = position()
    own_acc = jnp.zeros((ROWS, ROWS), F32)
    sib_acc = jnp.zeros((ROWS, ROWS), F32)
    for columns in column_steps(far.shape[1]):
        weight = coulomb[:, columns]
        ones = jnp.ones_like(weight)
        right = scaled(far[:, columns], jnp.where(even, ones, weight))
        own_acc += nt_dot(left[0:ROWS, columns], right)
        sib_acc += nt_dot(left[ROWS : 2 * ROWS, columns], right)
    biggest = jnp.maximum(jnp.max(jnp.abs(own_acc)), jnp.max(jnp.abs(sib_acc)))
    exponent = exponent_for(jnp.full((1, 1), biggest))
    factor = jnp.exp2(exponent)
    send_exponent(message, exponent)
    first = half == 0
    keep[...] = jnp.where(first, own_acc[0:HALF, :], own_acc[HALF:ROWS, :])
    message[0:HALF, 0:ROWS] = jnp.where(first, own_acc[HALF:ROWS, :], own_acc[0:HALF, :]) * factor
    mine = jnp.where(first, sib_acc[0:HALF, :], sib_acc[HALF:ROWS, :])
    other = jnp.where(first, sib_acc[HALF:ROWS, :], sib_acc[0:HALF, :])
    across[...] = mine
    corner[...] = jnp.where(first, other[:, 0:HALF], other[:, HALF:ROWS])
    message[0:HALF, ROWS : 2 * ROWS] = other * factor
    message[0:HALF, 2 * ROWS : 2 * ROWS + HALF] = (
        jnp.where(first, mine[:, HALF:ROWS], mine[:, 0:HALF]) * factor
    )


def sum_kernel(keep, across, corner, message, own_far, to_sib, to_far):
    _, half = position()
    first = half == 0
    own_far[...] = keep[...] + received(message, slice(0, ROWS))
    mine = across[...] + received(message, slice(ROWS, 2 * ROWS))
    to_sib[...] = mine
    other = (corner[...] + received(message, slice(2 * ROWS, 2 * ROWS + HALF))).T
    same = jnp.where(first, mine[:, 0:HALF], mine[:, HALF:ROWS]).T
    to_far[:, 0:HALF] = jnp.where(first, same, other)
    to_far[:, HALF:ROWS] = jnp.where(first, other, same)


def final_kernel(early, message, own_far, from_sib, from_far, out):
    even, _ = position()
    nearest = early[:, 0:ROWS] + received(message, slice(0, ROWS))
    inside = early[:, ROWS : 2 * ROWS] + received(message, slice(ROWS, 2 * ROWS))
    order = [from_far[...], own_far[...], nearest, inside, from_sib[...]]
    for at in range(5):
        out[:, at * ROWS : (at + 1) * ROWS] = jnp.where(even, order[at], order[4 - at])


def call(kernel, operands, outputs, on_chip=True):
    space = pltpu.MemorySpace.VMEM
    if on_chip:
        shapes = [space(shape, kind) for shape, kind in outputs]
    else:
        shapes = [jax.ShapeDtypeStruct(shape, kind) for shape, kind in outputs]
    return pl.pallas_call(
        kernel,
        in_specs=[pl.BlockSpec(memory_space=space)] * len(operands),
        out_specs=[pl.BlockSpec(memory_space=space)] * len(outputs),
        out_shape=shapes,
        compiler_params=pltpu.CompilerParams(vmem_limit_bytes=40 * 1024 * 1024),
    )(*[pltpu.with_memory_space_constraint(x, space) for x in operands])


def over_ga(value):
    return lax.ppermute(value.astype(F16), "ga", [(0, 1), (1, 0)]).astype(F32)


def shards(pair_density, coulomb):
    shard_points, pairs, waves = pair_density.shape
    width = shard_points * pairs
    count = lax.axis_size("ka")
    swap = [(i, i ^ 1) for i in range(count)]
    cross = [(i, (i - 1) % count if i % 2 == 0 else (i + 1) % count) for i in range(count)]
    factor = coulomb.reshape(1, waves)
    own = pair_density.reshape(width, waves)

    far = lax.ppermute(pair_density, "ka", cross)
    sib = lax.ppermute(pair_density, "ka", swap)
    far = far.reshape(width, waves)
    sib = sib.reshape(width, waves)
    early, early_message, left = call(
        early_kernel,
        (factor, own, sib),
        [((HALF, 2 * ROWS), F32), ((HALF + EXTRA, 2 * ROWS), F32), ((2 * ROWS, waves), BF16)],
    )
    early_message = over_ga(early_message)
    keep, across, corner, message = call(
        late_kernel,
        (factor, far, left),
        [
            ((HALF, ROWS), F32),
            ((HALF, ROWS), F32),
            ((HALF, HALF), F32),
            ((HALF + EXTRA, 2 * ROWS + HALF), F32),
        ],
    )
    own_far, to_sib, to_far = call(
        sum_kernel, (keep, across, corner, over_ga(message)), [((HALF, ROWS), F32)] * 3
    )
    from_far = lax.ppermute(to_far, "ka", cross)
    from_sib = lax.ppermute(to_sib, "ka", swap)
    (out,) = call(
        final_kernel,
        (early, early_message, own_far, from_sib, from_far),
        [((HALF, 5 * ROWS), F32)],
        on_chip=False,
    )
    return out


def solution(mesh):
    in_specs = (P("ka", None, "ga"), P("ga"))
    out_specs = P(("ka", "ga"), None)
    return jax.shard_map(shards, mesh=mesh, in_specs=in_specs, out_specs=out_specs, check_vma=False)
```

time: 138 us -> 82.6 us (0.60)
  the two profiles are of different devices: /device:TPU:40 before, /device:TPU:32 now
where the time goes in v2:
time: 82.6 us; the launch traced here: 82.3 us
  waiting for transfers between devices  42.8 us (52%)
  starting transfers between devices  31.3 us (38%)
  Pallas kernels  5.3 us (6%)
  local copies, waits for them, and re-layouts  2.62 us (3%)
    ppermute x1, waiting for transfers between devices, shards(): far = lax.ppermute(pair_density, 'ka', cross)  29.5 us
    ppermute x2, starting transfers between devices, over_ga(): return lax.ppermute(value.astype(F16), 'ga', [(0, 1), (1, 0)]).astype(F32)  12.4 us
    ppermute x1, starting transfers between devices, shards(): far = lax.ppermute(pair_density, 'ka', cross)  10.1 us
    ppermute x1, waiting for transfers between devices, shards(): from_far = lax.ppermute(to_far, 'ka', cross)  7.27 us
    ppermute x2, waiting for transfers between devices, over_ga(): return lax.ppermute(value.astype(F16), 'ga', [(0, 1), (1, 0)]).astype(F32)  6.03 us
    pallas_call x4, Pallas kernels, call(): pl.pallas_call(kernel, in_specs=[pl.BlockSpec(memory_space=space)] * len(...  5.3 us
    ppermute x1, starting transfers between devices, shards(): from_far = lax.ppermute(to_far, 'ka', cross)  4.98 us
    ppermute x1, starting transfers between devices, shards(): from_sib = lax.ppermute(to_sib, 'ka', swap)  1.92 us
  transfers between devices with their start and end apart: 6, of which 3 were waited for; matrix products, arithmetic and copies ran while one was open for 1% of the time, Pallas kernels for 3%

profile of v2, /device:TPU:32, one launch (start us, length us, event | category | flops | bytes accessed | tf_op | source)
XLA Modules:
  0.0 82.3 jit_solution(18422557810802918956)
XLA Ops:
  0.0 1.9 %collective-permute-start = (bf16[8,32,6016]{2,1,0:T(8,128)(2,1)}, bf16[8,32,6016]{2,1,0:T(8,128)(2,1)S(1)}, u32[]{:S(2)}, u32[]{:S(2)}) collective-permute-start(bf16[8,32,6016]{2,1,0:T(8,128)(2,1)} %param.2), channel_id=1, source_target_pairs={{0,2},{2,0},{4,6},{6,4},{8,10},{10,8},{12,14},{14,12},{16,18},{18,... | collective-permute-start | bytes 9240584 | tf_op jit(solution)/shard_map/ppermute | solution.py:152
  1.9 10.1 %collective-permute-start.2 = (bf16[8,32,6016]{2,1,0:T(8,128)(2,1)}, bf16[8,32,6016]{2,1,0:T(8,128)(2,1)S(1)}, u32[]{:S(2)}, u32[]{:S(2)}) collective-permute-start(bf16[8,32,6016]{2,1,0:T(8,128)(2,1)} %param.2), channel_id=1, source_target_pairs={{0,510},{2,4},{4,2},{6,8},{8,6},{10,12},{12,10},{14,16},{16,14},{1... | collective-permute-start | bytes 9240584 | tf_op jit(solution)/shard_map/ppermute | solution.py:151
  12.0 0.8 reshape.12.coulomb
  12.8 0.0 collective-permute-done
  12.8 0.0 copy-start
  12.8 1.9 %copy-done = bf16[8,32,6016]{2,1,0:T(8,128)(2,1)S(1)} copy-done((bf16[8,32,6016]{2,1,0:T(8,128)(2,1)S(1)}, bf16[8,32,6016]{2,1,0:T(8,128)(2,1)}, u32[]{:S(2)}) %copy-start) | copy-done | bytes 3080216
  14.7 2.3 %shard_map.28 = (f32[128,512]{1,0:T(8,128)S(1)}, f32[136,512]{1,0:T(8,128)S(1)}, bf16[512,6016]{1,0:T(8,128)(2,1)S(1)}) custom-call(f32[1,6016]{1,0:T(1,128)S(1)} %reshape.12.coulomb, bf16[256,6016]{1,0:T(8,128)(2,1)S(1)} %bitcast.4, bf16[256,6016]{1,0:T(8,128)(2,1)S(1)} %bitcast.5), custom_call_target="tpu_custom_call" | custom-call | tf_op jit(solution)/shard_map/pallas_call | solution.py:129
  16.9 29.5 %collective-permute-done.2 = bf16[8,32,6016]{2,1,0:T(8,128)(2,1)S(1)} collective-permute-done((bf16[8,32,6016]{2,1,0:T(8,128)(2,1)}, bf16[8,32,6016]{2,1,0:T(8,128)(2,1)S(1)}, u32[]{:S(2)}, u32[]{:S(2)}) %collective-permute-start.2) | collective-permute-done | bytes 3080224 | tf_op jit(solution)/shard_map/ppermute | solution.py:151
  46.5 2.0 %shard_map.29 = (f32[128,256]{1,0:T(8,128)S(1)}, f32[128,256]{1,0:T(8,128)S(1)}, f32[128,128]{1,0:T(8,128)S(1)}, f32[136,640]{1,0:T(8,128)S(1)}) custom-call(f32[1,6016]{1,0:T(1,128)S(1)} %reshape.12.coulomb, bf16[256,6016]{1,0:T(8,128)(2,1)S(1)} %bitcast.3, bf16[512,6016]{1,0:T(8,128)(2,1)S(1)} %get-tuple-element.17.left), custom_call_target="tpu_custom_call" | custom-call | tf_op jit(solution)/shard_map/pallas_call | solution.py:129
  48.5 10.5 %collective-permute-start.3 = (f16[136,640]{1,0:T(8,128)(2,1)S(1)}, f16[136,640]{1,0:T(8,128)(2,1)S(1)}, u32[]{:S(2)}, u32[]{:S(2)}) collective-permute-start(f16[136,640]{1,0:T(8,128)(2,1)S(1)} %convert_element_type.14), channel_id=1, source_target_pairs={{0,1},{1,0},{2,3},{3,2},{4,5},{5,4},{6,7},{7,6},{8,9},{9,8},{10,11... | collective-permute-start | bytes 522248 | tf_op jit(solution)/shard_map/ppermute | solution.py:139
  59.0 1.9 %collective-permute-start.1 = (f16[136,512]{1,0:T(8,128)(2,1)S(1)}, f16[136,512]{1,0:T(8,128)(2,1)S(1)}, u32[]{:S(2)}, u32[]{:S(2)}) collective-permute-start(f16[136,512]{1,0:T(8,128)(2,1)S(1)} %convert_element_type.12), channel_id=1, source_target_pairs={{0,1},{1,0},{2,3},{3,2},{4,5},{5,4},{6,7},{7,6},{8,9},{9,8},{10,11... | collective-permute-start | bytes 417800 | tf_op jit(solution)/shard_map/ppermute | solution.py:139
  61.0 6.0 %collective-permute-done.3 = f16[136,640]{1,0:T(8,128)(2,1)S(1)} collective-permute-done((f16[136,640]{1,0:T(8,128)(2,1)S(1)}, f16[136,640]{1,0:T(8,128)(2,1)S(1)}, u32[]{:S(2)}, u32[]{:S(2)}) %collective-permute-start.3) | collective-permute-done | bytes 174112 | tf_op jit(solution)/shard_map/ppermute | solution.py:139
  67.0 0.1 shard_map.30
  67.1 1.9 %collective-permute-start.4 = (f32[128,256]{1,0:T(8,128)S(1)}, f32[128,256]{1,0:T(8,128)S(1)}, u32[]{:S(2)}, u32[]{:S(2)}) collective-permute-start(f32[128,256]{1,0:T(8,128)S(1)} %get-tuple-element.23), channel_id=1, source_target_pairs={{0,2},{2,0},{4,6},{6,4},{8,10},{10,8},{12,14},{14,12},{16,18},{18,... | collective-permute-start | bytes 393224 | tf_op jit(solution)/shard_map/ppermute | solution.py:175
  69.0 5.0 %collective-permute-start.5 = (f32[128,256]{1,0:T(8,128)S(1)}, f32[128,256]{1,0:T(8,128)S(1)}, u32[]{:S(2)}, u32[]{:S(2)}) collective-permute-start(f32[128,256]{1,0:T(8,128)S(1)} %get-tuple-element.24), channel_id=1, source_target_pairs={{0,510},{2,4},{4,2},{6,8},{8,6},{10,12},{12,10},{14,16},{16,14},{1... | collective-permute-start | bytes 393224 | tf_op jit(solution)/shard_map/ppermute | solution.py:174
  74.0 0.0 collective-permute-done.1
  74.1 0.0 collective-permute-done.4.from_sib
  74.1 7.3 %collective-permute-done.5.from_far = f32[128,256]{1,0:T(8,128)S(1)} collective-permute-done((f32[128,256]{1,0:T(8,128)S(1)}, f32[128,256]{1,0:T(8,128)S(1)}, u32[]{:S(2)}, u32[]{:S(2)}) %collective-permute-start.5) | collective-permute-done | bytes 131104 | tf_op jit(solution)/shard_map/ppermute | solution.py:174
  81.4 0.9 %shard_map.31 = f32[128,1280]{1,0:T(8,128)} custom-call(f32[128,512]{1,0:T(8,128)S(1)} %get-tuple-element.15.early, f32[136,512]{1,0:T(8,128)S(1)} %convert_element_type.13.message, f32[128,256]{1,0:T(8,128)S(1)} %get-tuple-element.22.own_far, f32[128,256]{1,0:T(8,128)S(1)} %collective-permute-done.4.from_sib, f32[128,256]{1,0:T(8,128)S(1)} %collective-permute-done.5.from_far), custom_call_target="tpu_custom_call" | custom-call | tf_op jit(solution)/shard_map/pallas_call | solution.py:129
  (4 shorter events, 0.1 us)
Async XLA Ops:
  0.0 12.8 %collective-permute-start = (bf16[8,32,6016]{2,1,0:T(8,128)(2,1)}, bf16[8,32,6016]{2,1,0:T(8,128)(2,1)S(1)}, u32[]{:S(2)}, u32[]{:S(2)}) collective-permute-start(bf16[8,32,6016]{2,1,0:T(8,128)(2,1)} %param.2), channel_id=1, source_target_pairs={{0,2},{2,0},{4,6},{6,4},{8,10},{10,8},{12,14},{14,12},{16,18},{18,... | collective-permute-start | bytes 9240584 | tf_op jit(solution)/shard_map/ppermute | solution.py:152
  1.9 44.5 %collective-permute-start.2 = (bf16[8,32,6016]{2,1,0:T(8,128)(2,1)}, bf16[8,32,6016]{2,1,0:T(8,128)(2,1)S(1)}, u32[]{:S(2)}, u32[]{:S(2)}) collective-permute-start(bf16[8,32,6016]{2,1,0:T(8,128)(2,1)} %param.2), channel_id=1, source_target_pairs={{0,510},{2,4},{4,2},{6,8},{8,6},{10,12},{12,10},{14,16},{16,14},{1... | collective-permute-start | bytes 9240584 | tf_op jit(solution)/shard_map/ppermute | solution.py:151
  12.8 1.9 %copy-start = (bf16[8,32,6016]{2,1,0:T(8,128)(2,1)S(1)}, bf16[8,32,6016]{2,1,0:T(8,128)(2,1)}, u32[]{:S(2)}) copy-start(bf16[8,32,6016]{2,1,0:T(8,128)(2,1)} %param.2) | copy-start | bytes 9240580
  48.5 18.5 %collective-permute-start.3 = (f16[136,640]{1,0:T(8,128)(2,1)S(1)}, f16[136,640]{1,0:T(8,128)(2,1)S(1)}, u32[]{:S(2)}, u32[]{:S(2)}) collective-permute-start(f16[136,640]{1,0:T(8,128)(2,1)S(1)} %convert_element_type.14), channel_id=1, source_target_pairs={{0,1},{1,0},{2,3},{3,2},{4,5},{5,4},{6,7},{7,6},{8,9},{9,8},{10,11... | collective-permute-start | bytes 522248 | tf_op jit(solution)/shard_map/ppermute | solution.py:139
  59.0 15.0 %collective-permute-start.1 = (f16[136,512]{1,0:T(8,128)(2,1)S(1)}, f16[136,512]{1,0:T(8,128)(2,1)S(1)}, u32[]{:S(2)}, u32[]{:S(2)}) collective-permute-start(f16[136,512]{1,0:T(8,128)(2,1)S(1)} %convert_element_type.12), channel_id=1, source_target_pairs={{0,1},{1,0},{2,3},{3,2},{4,5},{5,4},{6,7},{7,6},{8,9},{9,8},{10,11... | collective-permute-start | bytes 417800 | tf_op jit(solution)/shard_map/ppermute | solution.py:139
  67.1 7.0 %collective-permute-start.4 = (f32[128,256]{1,0:T(8,128)S(1)}, f32[128,256]{1,0:T(8,128)S(1)}, u32[]{:S(2)}, u32[]{:S(2)}) collective-permute-start(f32[128,256]{1,0:T(8,128)S(1)} %get-tuple-element.23), channel_id=1, source_target_pairs={{0,2},{2,0},{4,6},{6,4},{8,10},{10,8},{12,14},{14,12},{16,18},{18,... | collective-permute-start | bytes 393224 | tf_op jit(solution)/shard_map/ppermute | solution.py:175
  69.0 12.3 %collective-permute-start.5 = (f32[128,256]{1,0:T(8,128)S(1)}, f32[128,256]{1,0:T(8,128)S(1)}, u32[]{:S(2)}, u32[]{:S(2)}) collective-permute-start(f32[128,256]{1,0:T(8,128)S(1)} %get-tuple-element.24), channel_id=1, source_target_pairs={{0,510},{2,4},{4,2},{6,8},{8,6},{10,12},{12,10},{14,16},{16,14},{1... | collective-permute-start | bytes 393224 | tf_op jit(solution)/shard_map/ppermute | solution.py:174

commit v3 on v2

v3 whole, which is shorter than its diff:
```python
import jax
import jax.numpy as jnp
from jax import lax
from jax.experimental import pallas as pl
from jax.experimental.pallas import tpu as pltpu
from jax.sharding import PartitionSpec as P


ROWS = 256
HALF = 128
EXTRA = 8
PEAK = 14.0
STEP = 512

F32 = jnp.float32
BF16 = jnp.bfloat16
F16 = jnp.float16


def nt_dot(left, right):
    return lax.dot_general(left, right, (((1,), (1,)), ((), ())), preferred_element_type=F32)


def column_steps(waves):
    return [slice(at, min(at + STEP, waves)) for at in range(0, waves, STEP)]


def scaled(piece, factor):
    return (piece.astype(F32) * factor).astype(BF16)


def position():
    return lax.axis_index("ka") % 2 == 0, lax.axis_index("ga")


def exponent_for(biggest):
    return PEAK - jnp.ceil(jnp.log2(jnp.maximum(biggest, 1e-30)))


def send_exponent(message, exponent):
    message[HALF : HALF + EXTRA, :] = jnp.broadcast_to(exponent, (EXTRA, message.shape[1]))


def received(message, columns):
    return message[0:HALF, columns] * jnp.exp2(-message[HALF : HALF + 1, columns])


def halves(block, half):
    top, bottom = block[0:HALF, :], block[HALF:ROWS, :]
    first = half == 0
    return jnp.where(first, top, bottom), jnp.where(first, bottom, top)


def early_kernel(coulomb, own, sib, keep, give, left):
    even, half = position()
    own_acc = jnp.zeros((ROWS, ROWS), F32)
    sib_acc = jnp.zeros((ROWS, ROWS), F32)
    for columns in column_steps(own.shape[1]):
        weight = coulomb[:, columns]
        ones = jnp.ones_like(weight)
        near = jnp.where(even, ones, weight)
        away = jnp.where(even, weight, ones)
        mine = own[:, columns]
        other = sib[:, columns]
        other_away = scaled(other, away)
        own_acc += nt_dot(scaled(mine, weight), mine)
        sib_acc += nt_dot(scaled(mine, near), other_away)
        left[0:ROWS, columns] = scaled(mine, away)
        left[ROWS : 2 * ROWS, columns] = other_away
    keep[:, 0:ROWS], give[:, 0:ROWS] = halves(own_acc, half)
    keep[:, ROWS : 2 * ROWS], give[:, ROWS : 2 * ROWS] = halves(sib_acc, half)


def across_kernel(coulomb, far, left, across, corner, message, right):
    even, half = position()
    acc = jnp.zeros((ROWS, ROWS), F32)
    for columns in column_steps(far.shape[1]):
        weight = coulomb[:, columns]
        piece = scaled(far[:, columns], jnp.where(even, jnp.ones_like(weight), weight))
        right[:, columns] = piece
        acc += nt_dot(left[ROWS : 2 * ROWS, columns], piece)
    exponent = exponent_for(jnp.full((1, 1), jnp.max(jnp.abs(acc))))
    factor = jnp.exp2(exponent)
    send_exponent(message, exponent)
    first = half == 0
    mine, other = halves(acc, half)
    across[...] = mine
    corner[...] = jnp.where(first, other[:, 0:HALF], other[:, HALF:ROWS])
    message[0:HALF, 0:ROWS] = other * factor
    message[0:HALF, ROWS : ROWS + HALF] = jnp.where(first, mine[:, HALF:ROWS], mine[:, 0:HALF]) * factor


def beside_kernel(right, left, give, keep, message):
    _, half = position()
    acc = nt_dot(left[0:ROWS, :], right[...])
    early = give[...]
    biggest = jnp.maximum(jnp.max(jnp.abs(acc)), jnp.max(jnp.abs(early)))
    exponent = exponent_for(jnp.full((1, 1), biggest))
    factor = jnp.exp2(exponent)
    send_exponent(message, exponent)
    keep[...], other = halves(acc, half)
    message[0:HALF, 0:ROWS] = other * factor
    message[0:HALF, ROWS : 3 * ROWS] = early * factor


def sum_kernel(across, corner, message, to_sib, to_far):
    _, half = position()
    first = half == 0
    mine = across[...] + received(message, slice(0, ROWS))
    other = (corner[...] + received(message, slice(ROWS, ROWS + HALF))).T
    same = jnp.where(first, mine[:, 0:HALF], mine[:, HALF:ROWS]).T
    biggest = jnp.maximum(jnp.max(jnp.abs(mine)), jnp.max(jnp.abs(other)))
    exponent = exponent_for(jnp.full((1, 1), biggest))
    factor = jnp.exp2(exponent)
    send_exponent(to_sib, exponent)
    send_exponent(to_far, exponent)
    to_sib[0:HALF, :] = mine * factor
    to_far[0:HALF, 0:HALF] = jnp.where(first, same, other) * factor
    to_far[0:HALF, HALF:ROWS] = jnp.where(first, other, same) * factor


def final_kernel(early, beside, message, from_sib, from_far, out):
    even, _ = position()
    own_far = beside[...] + received(message, slice(0, ROWS))
    nearest = early[:, 0:ROWS] + received(message, slice(ROWS, 2 * ROWS))
    inside = early[:, ROWS : 2 * ROWS] + received(message, slice(2 * ROWS, 3 * ROWS))
    whole = slice(0, ROWS)
    order = [received(from_far, whole), own_far, nearest, inside, received(from_sib, whole)]
    for at in range(5):
        out[:, at * ROWS : (at + 1) * ROWS] = jnp.where(even, order[at], order[4 - at])


def call(kernel, operands, outputs, on_chip=True):
    space = pltpu.MemorySpace.VMEM
    if on_chip:
        shapes = [space(shape, kind) for shape, kind in outputs]
    else:
        shapes = [jax.ShapeDtypeStruct(shape, kind) for shape, kind in outputs]
    return pl.pallas_call(
        kernel,
        in_specs=[pl.BlockSpec(memory_space=space)] * len(operands),
        out_specs=[pl.BlockSpec(memory_space=space)] * len(outputs),
        out_shape=shapes,
        compiler_params=pltpu.CompilerParams(vmem_limit_bytes=40 * 1024 * 1024),
    )(*[pltpu.with_memory_space_constraint(x, space) for x in operands])


def sent(value, axes, pairs):
    return lax.ppermute(value.astype(F16), axes, pairs).astype(F32)


def over_ga(value):
    return sent(value, "ga", [(0, 1), (1, 0)])


def shards(pair_density, coulomb):
    shard_points, pairs, waves = pair_density.shape
    width = shard_points * pairs
    count = lax.axis_size("ka")
    swap = [(i, i ^ 1) for i in range(count)]
    cross = [(i, (i - 1) % count if i % 2 == 0 else (i + 1) % count) for i in range(count)]
    factor = coulomb.reshape(1, waves)
    own = pair_density.reshape(width, waves)

    far = lax.ppermute(pair_density, "ka", cross)
    sib = lax.ppermute(pair_density, "ka", swap)
    far = far.reshape(width, waves)
    sib = sib.reshape(width, waves)
    early, give, left = call(
        early_kernel,
        (factor, own, sib),
        [((HALF, 2 * ROWS), F32), ((HALF, 2 * ROWS), F32), ((2 * ROWS, waves), BF16)],
    )
    across, corner, message, right = call(
        across_kernel,
        (factor, far, left),
        [
            ((HALF, ROWS), F32),
            ((HALF, HALF), F32),
            ((HALF + EXTRA, ROWS + HALF), F32),
            ((ROWS, waves), BF16),
        ],
    )
    message = over_ga(message)
    beside, rest = call(
        beside_kernel, (right, left, give), [((HALF, ROWS), F32), ((HALF + EXTRA, 3 * ROWS), F32)]
    )
    rest = over_ga(rest)
    to_sib, to_far = call(sum_kernel, (across, corner, message), [((HALF + EXTRA, ROWS), F32)] * 2)
    from_far = sent(to_far, "ka", cross)
    from_sib = sent(to_sib, "ka", swap)
    (out,) = call(
        final_kernel,
        (early, beside, rest, from_sib, from_far),
        [((HALF, 5 * ROWS), F32)],
        on_chip=False,
    )
    return out


def solution(mesh):
    in_specs = (P("ka", None, "ga"), P("ga"))
    out_specs = P(("ka", "ga"), None)
    return jax.shard_map(shards, mesh=mesh, in_specs=in_specs, out_specs=out_specs, check_vma=False)
```

time: 82.6 us -> 86.6 us (1.048)
  the two profiles are of different devices: /device:TPU:32 before, /device:TPU:1 now
where the time goes in v3:
time: 86.6 us; the launch traced here: 86.2 us
  starting transfers between devices  39 us (45%)
  waiting for transfers between devices  38.5 us (44%)
  Pallas kernels  5.81 us (7%)
  local copies, waits for them, and re-layouts  2.63 us (3%)
    ppermute x1, waiting for transfers between devices, shards(): far = lax.ppermute(pair_density, 'ka', cross)  29 us
    ppermute x4, starting transfers between devices, sent(): return lax.ppermute(value.astype(F16), axes, pairs).astype(F32)  28.3 us
    ppermute x1, starting transfers between devices, shards(): sib = lax.ppermute(pair_density, 'ka', swap)  8.74 us
    ppermute x4, waiting for transfers between devices, sent(): return lax.ppermute(value.astype(F16), axes, pairs).astype(F32)  6.83 us
    pallas_call x5, Pallas kernels, call(): pl.pallas_call(kernel, in_specs=[pl.BlockSpec(memory_space=space)] * len(...  5.81 us
    ppermute x1, waiting for transfers between devices, shards(): sib = lax.ppermute(pair_density, 'ka', swap)  2.69 us
    ppermute x1, starting transfers between devices, shards(): far = lax.ppermute(pair_density, 'ka', cross)  1.92 us
    unnamed x2, local copies, waits for them, and re-layouts  1.87 us
  transfers between devices with their start and end apart: 6, of which 4 were waited for; matrix products, arithmetic and copies ran while one was open for 1% of the time, Pallas kernels for 3%

profile of v3, /device:TPU:1, one launch (start us, length us, event | category | flops | bytes accessed | tf_op | source)
XLA Modules:
  0.0 86.2 jit_solution(14291898796728476999)
XLA Ops:
  0.0 8.7 %collective-permute-start = (bf16[8,32,6016]{2,1,0:T(8,128)(2,1)}, bf16[8,32,6016]{2,1,0:T(8,128)(2,1)S(1)}, u32[]{:S(2)}, u32[]{:S(2)}) collective-permute-start(bf16[8,32,6016]{2,1,0:T(8,128)(2,1)} %param.2), channel_id=1, source_target_pairs={{0,2},{2,0},{4,6},{6,4},{8,10},{10,8},{12,14},{14,12},{16,18},{18,... | collective-permute-start | bytes 9240584 | tf_op jit(solution)/shard_map/ppermute | solution.py:166
  8.7 1.9 %collective-permute-start.1 = (bf16[8,32,6016]{2,1,0:T(8,128)(2,1)}, bf16[8,32,6016]{2,1,0:T(8,128)(2,1)S(1)}, u32[]{:S(2)}, u32[]{:S(2)}) collective-permute-start(bf16[8,32,6016]{2,1,0:T(8,128)(2,1)} %param.2), channel_id=1, source_target_pairs={{0,510},{2,4},{4,2},{6,8},{8,6},{10,12},{12,10},{14,16},{16,14},{1... | collective-permute-start | bytes 9240584 | tf_op jit(solution)/shard_map/ppermute | solution.py:165
  10.7 0.8 reshape.12.coulomb
  11.4 2.7 %collective-permute-done = bf16[8,32,6016]{2,1,0:T(8,128)(2,1)S(1)} collective-permute-done((bf16[8,32,6016]{2,1,0:T(8,128)(2,1)}, bf16[8,32,6016]{2,1,0:T(8,128)(2,1)S(1)}, u32[]{:S(2)}, u32[]{:S(2)}) %collective-permute-start) | collective-permute-done | bytes 3080224 | tf_op jit(solution)/shard_map/ppermute | solution.py:166
  14.1 0.0 copy-start
  14.1 1.9 %copy-done = bf16[8,32,6016]{2,1,0:T(8,128)(2,1)S(1)} copy-done((bf16[8,32,6016]{2,1,0:T(8,128)(2,1)S(1)}, bf16[8,32,6016]{2,1,0:T(8,128)(2,1)}, u32[]{:S(2)}) %copy-start) | copy-done | bytes 3080216
  16.0 2.1 %shard_map.28 = (f32[128,512]{1,0:T(8,128)S(1)}, f32[128,512]{1,0:T(8,128)S(1)}, bf16[512,6016]{1,0:T(8,128)(2,1)S(1)}) custom-call(f32[1,6016]{1,0:T(1,128)S(1)} %reshape.12.coulomb, bf16[256,6016]{1,0:T(8,128)(2,1)S(1)} %bitcast.4, bf16[256,6016]{1,0:T(8,128)(2,1)S(1)} %bitcast.5), custom_call_target="tpu_custom_call" | custom-call | tf_op jit(solution)/shard_map/pallas_call | solution.py:139
  18.1 29.0 %collective-permute-done.1 = bf16[8,32,6016]{2,1,0:T(8,128)(2,1)S(1)} collective-permute-done((bf16[8,32,6016]{2,1,0:T(8,128)(2,1)}, bf16[8,32,6016]{2,1,0:T(8,128)(2,1)S(1)}, u32[]{:S(2)}, u32[]{:S(2)}) %collective-permute-start.1) | collective-permute-done | bytes 3080224 | tf_op jit(solution)/shard_map/ppermute | solution.py:165
  47.1 1.3 %shard_map.29 = (f32[128,256]{1,0:T(8,128)S(1)}, f32[128,128]{1,0:T(8,128)S(1)}, f32[136,384]{1,0:T(8,128)S(1)}, bf16[256,6016]{1,0:T(8,128)(2,1)S(1)}) custom-call(f32[1,6016]{1,0:T(1,128)S(1)} %reshape.12.coulomb, bf16[256,6016]{1,0:T(8,128)(2,1)S(1)} %bitcast.3, bf16[512,6016]{1,0:T(8,128)(2,1)S(1)} %get-tuple-element.17.left), custom_call_target="tpu_custom_call" | custom-call | tf_op jit(solution)/shard_map/pallas_call | solution.py:139
  48.5 1.2 %shard_map.30 = (f32[128,256]{1,0:T(8,128)S(1)}, f32[136,768]{1,0:T(8,128)S(1)}) custom-call(bf16[256,6016]{1,0:T(8,128)(2,1)S(1)} %get-tuple-element.18.right, bf16[512,6016]{1,0:T(8,128)(2,1)S(1)} %get-tuple-element.17.left, f32[128,512]{1,0:T(8,128)S(1)} %get-tuple-element.19.give), custom_call_target="tpu_custom_call" | custom-call | tf_op jit(solution)/shard_map/pallas_call | solution.py:139
  49.7 5.3 %collective-permute-start.2 = (f16[136,768]{1,0:T(8,128)(2,1)S(1)}, f16[136,768]{1,0:T(8,128)(2,1)S(1)}, u32[]{:S(2)}, u32[]{:S(2)}) collective-permute-start(f16[136,768]{1,0:T(8,128)(2,1)S(1)} %convert_element_type.24), channel_id=1, source_target_pairs={{0,1},{1,0},{2,3},{3,2},{4,5},{5,4},{6,7},{7,6},{8,9},{9,8},{10,11... | collective-permute-start | bytes 626696 | tf_op jit(solution)/shard_map/ppermute | solution.py:149
  55.0 3.9 %collective-permute-start.3 = (f16[136,384]{1,0:T(8,128)(2,1)S(1)}, f16[136,384]{1,0:T(8,128)(2,1)S(1)}, u32[]{:S(2)}, u32[]{:S(2)}) collective-permute-start(f16[136,384]{1,0:T(8,128)(2,1)S(1)} %convert_element_type.26), channel_id=1, source_target_pairs={{0,1},{1,0},{2,3},{3,2},{4,5},{5,4},{6,7},{7,6},{8,9},{9,8},{10,11... | collective-permute-start | bytes 313352 | tf_op jit(solution)/shard_map/ppermute | solution.py:149
  58.9 6.0 %collective-permute-done.3 = f16[136,384]{1,0:T(8,128)(2,1)S(1)} collective-permute-done((f16[136,384]{1,0:T(8,128)(2,1)S(1)}, f16[136,384]{1,0:T(8,128)(2,1)S(1)}, u32[]{:S(2)}, u32[]{:S(2)}) %collective-permute-start.3) | collective-permute-done | bytes 104480 | tf_op jit(solution)/shard_map/ppermute | solution.py:149
  64.9 0.3 shard_map.31
  65.2 4.1 %collective-permute-start.5 = (f16[136,256]{1,0:T(8,128)(2,1)S(1)}, f16[136,256]{1,0:T(8,128)(2,1)S(1)}, u32[]{:S(2)}, u32[]{:S(2)}) collective-permute-start(f16[136,256]{1,0:T(8,128)(2,1)S(1)} %convert_element_type.30), channel_id=1, source_target_pairs={{0,510},{2,4},{4,2},{6,8},{8,6},{10,12},{12,10},{14,16},{16,14},{1... | collective-permute-start | bytes 208904 | tf_op jit(solution)/shard_map/ppermute | solution.py:149
  69.3 15.0 %collective-permute-start.4 = (f16[136,256]{1,0:T(8,128)(2,1)S(1)}, f16[136,256]{1,0:T(8,128)(2,1)S(1)}, u32[]{:S(2)}, u32[]{:S(2)}) collective-permute-start(f16[136,256]{1,0:T(8,128)(2,1)S(1)} %convert_element_type.28), channel_id=1, source_target_pairs={{0,2},{2,0},{4,6},{6,4},{8,10},{10,8},{12,14},{14,12},{16,18},{18,... | collective-permute-start | bytes 208904 | tf_op jit(solution)/shard_map/ppermute | solution.py:149
  84.3 0.0 collective-permute-done.5
  84.4 0.9 collective-permute-done.4
  85.2 0.0 collective-permute-done.2
  85.3 0.9 %shard_map.32 = f32[128,1280]{1,0:T(8,128)} custom-call(f32[128,512]{1,0:T(8,128)S(1)} %get-tuple-element.16.early, f32[128,256]{1,0:T(8,128)S(1)} %get-tuple-element.20.beside, f32[136,768]{1,0:T(8,128)S(1)} %convert_element_type.25.message, f32[136,256]{1,0:T(8,128)S(1)} %convert_element_type.29.from_sib, f32[136,256]{1,0:T(8,128)S(1)} %convert_element_type.31.from_far), custom_call_target="tpu_custom_call" | custom-call | tf_op jit(solution)/shard_map/pallas_call | solution.py:139
  (8 shorter events, 0.1 us)
Async XLA Ops:
  0.0 14.1 %collective-permute-start = (bf16[8,32,6016]{2,1,0:T(8,128)(2,1)}, bf16[8,32,6016]{2,1,0:T(8,128)(2,1)S(1)}, u32[]{:S(2)}, u32[]{:S(2)}) collective-permute-start(bf16[8,32,6016]{2,1,0:T(8,128)(2,1)} %param.2), channel_id=1, source_target_pairs={{0,2},{2,0},{4,6},{6,4},{8,10},{10,8},{12,14},{14,12},{16,18},{18,... | collective-permute-start | bytes 9240584 | tf_op jit(solution)/shard_map/ppermute | solution.py:166
  8.7 38.4 %collective-permute-start.1 = (bf16[8,32,6016]{2,1,0:T(8,128)(2,1)}, bf16[8,32,6016]{2,1,0:T(8,128)(2,1)S(1)}, u32[]{:S(2)}, u32[]{:S(2)}) collective-permute-start(bf16[8,32,6016]{2,1,0:T(8,128)(2,1)} %param.2), channel_id=1, source_target_pairs={{0,510},{2,4},{4,2},{6,8},{8,6},{10,12},{12,10},{14,16},{16,14},{1... | collective-permute-start | bytes 9240584 | tf_op jit(solution)/shard_map/ppermute | solution.py:165
  14.1 1.9 %copy-start = (bf16[8,32,6016]{2,1,0:T(8,128)(2,1)S(1)}, bf16[8,32,6016]{2,1,0:T(8,128)(2,1)}, u32[]{:S(2)}) copy-start(bf16[8,32,6016]{2,1,0:T(8,128)(2,1)} %param.2) | copy-start | bytes 9240580
  49.7 35.6 %collective-permute-start.2 = (f16[136,768]{1,0:T(8,128)(2,1)S(1)}, f16[136,768]{1,0:T(8,128)(2,1)S(1)}, u32[]{:S(2)}, u32[]{:S(2)}) collective-permute-start(f16[136,768]{1,0:T(8,128)(2,1)S(1)} %convert_element_type.24), channel_id=1, source_target_pairs={{0,1},{1,0},{2,3},{3,2},{4,5},{5,4},{6,7},{7,6},{8,9},{9,8},{10,11... | collective-permute-start | bytes 626696 | tf_op jit(solution)/shard_map/ppermute | solution.py:149
  55.0 9.9 %collective-permute-start.3 = (f16[136,384]{1,0:T(8,128)(2,1)S(1)}, f16[136,384]{1,0:T(8,128)(2,1)S(1)}, u32[]{:S(2)}, u32[]{:S(2)}) collective-permute-start(f16[136,384]{1,0:T(8,128)(2,1)S(1)} %convert_element_type.26), channel_id=1, source_target_pairs={{0,1},{1,0},{2,3},{3,2},{4,5},{5,4},{6,7},{7,6},{8,9},{9,8},{10,11... | collective-permute-start | bytes 313352 | tf_op jit(solution)/shard_map/ppermute | solution.py:149
  65.2 19.2 %collective-permute-start.5 = (f16[136,256]{1,0:T(8,128)(2,1)S(1)}, f16[136,256]{1,0:T(8,128)(2,1)S(1)}, u32[]{:S(2)}, u32[]{:S(2)}) collective-permute-start(f16[136,256]{1,0:T(8,128)(2,1)S(1)} %convert_element_type.30), channel_id=1, source_target_pairs={{0,510},{2,4},{4,2},{6,8},{8,6},{10,12},{12,10},{14,16},{16,14},{1... | collective-permute-start | bytes 208904 | tf_op jit(solution)/shard_map/ppermute | solution.py:149
  69.3 15.9 %collective-permute-start.4 = (f16[136,256]{1,0:T(8,128)(2,1)S(1)}, f16[136,256]{1,0:T(8,128)(2,1)S(1)}, u32[]{:S(2)}, u32[]{:S(2)}) collective-permute-start(f16[136,256]{1,0:T(8,128)(2,1)S(1)} %convert_element_type.28), channel_id=1, source_target_pairs={{0,2},{2,0},{4,6},{6,4},{8,10},{10,8},{12,14},{14,12},{16,18},{18,... | collective-permute-start | bytes 208904 | tf_op jit(solution)/shard_map/ppermute | solution.py:149

commit v4 on v3

--- a/solution.py
+++ b/solution.py
@@ -35,6 +35,10 @@
 
 def exponent_for(biggest):
     return PEAK - jnp.ceil(jnp.log2(jnp.maximum(biggest, 1e-30)))
+
+
+def common_exponent(given, message):
+    return jnp.minimum(given[HALF : HALF + 1, 0:1], message[HALF : HALF + 1, 0:1])
 
 
 def send_exponent(message, exponent):
@@ -71,13 +75,12 @@
     keep[:, ROWS : 2 * ROWS], give[:, ROWS : 2 * ROWS] = halves(sib_acc, half)
 
 
-def across_kernel(coulomb, far, left, across, corner, message, right):
+def across_kernel(coulomb, far, left, across, corner, message):
     even, half = position()
     acc = jnp.zeros((ROWS, ROWS), F32)
     for columns in column_steps(far.shape[1]):
         weight = coulomb[:, columns]
         piece = scaled(far[:, columns], jnp.where(even, jnp.ones_like(weight), weight))
-        right[:, columns] = piece
         acc += nt_dot(left[ROWS : 2 * ROWS, columns], piece)
     exponent = exponent_for(jnp.full((1, 1), jnp.max(jnp.abs(acc))))
     factor = jnp.exp2(exponent)
@@ -90,9 +93,13 @@
     message[0:HALF, ROWS : ROWS + HALF] = jnp.where(first, mine[:, HALF:ROWS], mine[:, 0:HALF]) * factor
 
 
-def beside_kernel(right, left, give, keep, message):
-    _, half = position()
-    acc = nt_dot(left[0:ROWS, :], right[...])
+def beside_kernel(coulomb, far, left, give, keep, message):
+    even, half = position()
+    acc = jnp.zeros((ROWS, ROWS), F32)
+    for columns in column_steps(far.shape[1]):
+        weight = coulomb[:, columns]
+        piece = scaled(far[:, columns], jnp.where(even, jnp.ones_like(weight), weight))
+        acc += nt_dot(left[0:ROWS, columns], piece)
     early = give[...]
     biggest = jnp.maximum(jnp.max(jnp.abs(acc)), jnp.max(jnp.abs(early)))
     exponent = exponent_for(jnp.full((1, 1), biggest))
@@ -103,14 +110,13 @@
     message[0:HALF, ROWS : 3 * ROWS] = early * factor
 
 
-def sum_kernel(across, corner, message, to_sib, to_far):
+def sum_kernel(across, corner, given, message, to_sib, to_far):
     _, half = position()
     first = half == 0
     mine = across[...] + received(message, slice(0, ROWS))
     other = (corner[...] + received(message, slice(ROWS, ROWS + HALF))).T
     same = jnp.where(first, mine[:, 0:HALF], mine[:, HALF:ROWS]).T
-    biggest = jnp.maximum(jnp.max(jnp.abs(mine)), jnp.max(jnp.abs(other)))
-    exponent = exponent_for(jnp.full((1, 1), biggest))
+    exponent = common_exponent(given, message)
     factor = jnp.exp2(exponent)
     send_exponent(to_sib, exponent)
     send_exponent(to_far, exponent)
@@ -119,30 +125,63 @@
     to_far[0:HALF, HALF:ROWS] = jnp.where(first, other, same) * factor
 
 
-def final_kernel(early, beside, message, from_sib, from_far, out):
+def middle_kernel(early, beside, message, out, blocks, done):
     even, _ = position()
     own_far = beside[...] + received(message, slice(0, ROWS))
-    nearest = early[:, 0:ROWS] + received(message, slice(ROWS, 2 * ROWS))
     inside = early[:, ROWS : 2 * ROWS] + received(message, slice(2 * ROWS, 3 * ROWS))
+    blocks[:, 0:ROWS] = jnp.where(even, own_far, inside)
+    blocks[:, ROWS : 2 * ROWS] = early[:, 0:ROWS] + received(message, slice(ROWS, 2 * ROWS))
+    blocks[:, 2 * ROWS : 3 * ROWS] = jnp.where(even, inside, own_far)
+    copy = pltpu.make_async_copy(blocks, out.at[:, ROWS : 4 * ROWS], done)
+    copy.start()
+    copy.wait()
+
+
+def ends_kernel(from_sib, from_far, filled, out, low, high, low_done, high_done):
+    del filled
+    even, _ = position()
     whole = slice(0, ROWS)
-    order = [received(from_far, whole), own_far, nearest, inside, received(from_sib, whole)]
-    for at in range(5):
-        out[:, at * ROWS : (at + 1) * ROWS] = jnp.where(even, order[at], order[4 - at])
-
-
-def call(kernel, operands, outputs, on_chip=True):
+    sib_block = received(from_sib, whole)
+    far_block = received(from_far, whole)
+    low[...] = jnp.where(even, far_block, sib_block)
+    low_copy = pltpu.make_async_copy(low, out.at[:, 0:ROWS], low_done)
+    low_copy.start()
+    high[...] = jnp.where(even, sib_block, far_block)
+    high_copy = pltpu.make_async_copy(high, out.at[:, 4 * ROWS : 5 * ROWS], high_done)
+    high_copy.start()
+    low_copy.wait()
+    high_copy.wait()
+
+
+def call(kernel, operands, outputs):
     space = pltpu.MemorySpace.VMEM
-    if on_chip:
-        shapes = [space(shape, kind) for shape, kind in outputs]
-    else:
-        shapes = [jax.ShapeDtypeStruct(shape, kind) for shape, kind in outputs]
     return pl.pallas_call(
         kernel,
         in_specs=[pl.BlockSpec(memory_space=space)] * len(operands),
         out_specs=[pl.BlockSpec(memory_space=space)] * len(outputs),
-        out_shape=shapes,
+        out_shape=[space(shape, kind) for shape, kind in outputs],
         compiler_params=pltpu.CompilerParams(vmem_limit_bytes=40 * 1024 * 1024),
     )(*[pltpu.with_memory_space_constraint(x, space) for x in operands])
+
+
+def write_out(kernel, operands, widths, filled=None):
+    space = pltpu.MemorySpace.VMEM
+    held = [pltpu.with_memory_space_constraint(x, space) for x in operands]
+    specs = [pl.BlockSpec(memory_space=space)] * len(held)
+    aliases = {}
+    if filled is not None:
+        aliases = {len(held): 0}
+        held.append(filled)
+        specs.append(pl.BlockSpec(memory_space=pl.ANY))
+    return pl.pallas_call(
+        kernel,
+        in_specs=specs,
+        out_specs=pl.BlockSpec(memory_space=pl.ANY),
+        out_shape=jax.ShapeDtypeStruct((HALF, 5 * ROWS), F32),
+        scratch_shapes=[pltpu.VMEM((HALF, width), F32) for width in widths]
+        + [pltpu.SemaphoreType.DMA] * len(widths),
+        input_output_aliases=aliases,
+    )(*held)
 
 
 def sent(value, axes, pairs):
@@ -171,31 +210,29 @@
         (factor, own, sib),
         [((HALF, 2 * ROWS), F32), ((HALF, 2 * ROWS), F32), ((2 * ROWS, waves), BF16)],
     )
-    across, corner, message, right = call(
+    across, corner, message = call(
         across_kernel,
         (factor, far, left),
         [
             ((HALF, ROWS), F32),
             ((HALF, HALF), F32),
             ((HALF + EXTRA, ROWS + HALF), F32),
-            ((ROWS, waves), BF16),
         ],
     )
-    message = over_ga(message)
+    taken = over_ga(message)
     beside, rest = call(
-        beside_kernel, (right, left, give), [((HALF, ROWS), F32), ((HALF + EXTRA, 3 * ROWS), F32)]
+        beside_kernel,
+        (factor, far, left, give),
+        [((HALF, ROWS), F32), ((HALF + EXTRA, 3 * ROWS), F32)],
     )
     rest = over_ga(rest)
-    to_sib, to_far = call(sum_kernel, (across, corner, message), [((HALF + EXTRA, ROWS), F32)] * 2)
+    to_sib, to_far = call(
+        sum_kernel, (across, corner, message, taken), [((HALF + EXTRA, ROWS), F32)] * 2
+    )
     from_far = sent(to_far, "ka", cross)
     from_sib = sent(to_sib, "ka", swap)
-    (out,) = call(
-        final_kernel,
-        (early, beside, rest, from_sib, from_far),
-        [((HALF, 5 * ROWS), F32)],
-        on_chip=False,
-    )
-    return out
+    out = write_out(middle_kernel, (early, beside, rest), (3 * ROWS,))
+    return write_out(ends_kernel, (from_sib, from_far), (ROWS, ROWS), out)
 
 
 def solution(mesh):

time: 86.6 us -> 86.4 us (level)
  the two profiles are of different devices: /device:TPU:1 before, /device:TPU:56 now
where the time goes in v4:
time: 86.4 us; the launch traced here: 86 us
  waiting for transfers between devices  46.4 us (54%)
  starting transfers between devices  30.4 us (35%)
  Pallas kernels  6.2 us (7%)
  local copies, waits for them, and re-layouts  2.62 us (3%)
    ppermute x1, waiting for transfers between devices, shards(): far = lax.ppermute(pair_density, 'ka', cross)  29.7 us
    ppermute x4, starting transfers between devices, sent(): return lax.ppermute(value.astype(F16), axes, pairs).astype(F32)  17.6 us
    ppermute x4, waiting for transfers between devices, sent(): return lax.ppermute(value.astype(F16), axes, pairs).astype(F32)  16.8 us
    ppermute x1, starting transfers between devices, shards(): far = lax.ppermute(pair_density, 'ka', cross)  11 us
    pallas_call x4, Pallas kernels, call(): pl.pallas_call(kernel, in_specs=[pl.BlockSpec(memory_space=space)] * len(...  4.64 us
    ppermute x1, starting transfers between devices, shards(): sib = lax.ppermute(pair_density, 'ka', swap)  1.91 us
    unnamed x2, local copies, waits for them, and re-layouts  1.87 us
  transfers between devices with their start and end apart: 6, of which 3 were waited for; matrix products, arithmetic and copies ran while one was open for 1% of the time, Pallas kernels for 4%

profile of v4, /device:TPU:56, one launch (start us, length us, event | category | flops | bytes accessed | tf_op | source)
XLA Modules:
  0.0 86.0 jit_solution(2209143732642733838)
XLA Ops:
  0.0 1.9 %collective-permute-start.1 = (bf16[8,32,6016]{2,1,0:T(8,128)(2,1)}, bf16[8,32,6016]{2,1,0:T(8,128)(2,1)S(1)}, u32[]{:S(2)}, u32[]{:S(2)}) collective-permute-start(bf16[8,32,6016]{2,1,0:T(8,128)(2,1)} %param.2), channel_id=1, source_target_pairs={{0,2},{2,0},{4,6},{6,4},{8,10},{10,8},{12,14},{14,12},{16,18},{18,... | collective-permute-start | bytes 9240584 | tf_op jit(solution)/shard_map/ppermute | solution.py:205
  1.9 11.0 %collective-permute-start = (bf16[8,32,6016]{2,1,0:T(8,128)(2,1)}, bf16[8,32,6016]{2,1,0:T(8,128)(2,1)S(1)}, u32[]{:S(2)}, u32[]{:S(2)}) collective-permute-start(bf16[8,32,6016]{2,1,0:T(8,128)(2,1)} %param.2), channel_id=1, source_target_pairs={{0,510},{2,4},{4,2},{6,8},{8,6},{10,12},{12,10},{14,16},{16,14},{1... | collective-permute-start | bytes 9240584 | tf_op jit(solution)/shard_map/ppermute | solution.py:204
  12.9 0.8 reshape.12.coulomb
  13.7 0.0 collective-permute-done.1
  13.7 0.0 copy-start
  13.7 1.9 %copy-done = bf16[8,32,6016]{2,1,0:T(8,128)(2,1)S(1)} copy-done((bf16[8,32,6016]{2,1,0:T(8,128)(2,1)S(1)}, bf16[8,32,6016]{2,1,0:T(8,128)(2,1)}, u32[]{:S(2)}) %copy-start) | copy-done | bytes 3080216
  15.6 2.1 %shard_map.28 = (f32[128,512]{1,0:T(8,128)S(1)}, f32[128,512]{1,0:T(8,128)S(1)}, bf16[512,6016]{1,0:T(8,128)(2,1)S(1)}) custom-call(f32[1,6016]{1,0:T(1,128)S(1)} %reshape.12.coulomb, bf16[256,6016]{1,0:T(8,128)(2,1)S(1)} %bitcast.5, bf16[256,6016]{1,0:T(8,128)(2,1)S(1)} %bitcast.6), custom_call_target="tpu_custom_call" | custom-call | tf_op jit(solution)/shard_map/pallas_call | solution.py:158
  17.7 29.7 %collective-permute-done = bf16[8,32,6016]{2,1,0:T(8,128)(2,1)S(1)} collective-permute-done((bf16[8,32,6016]{2,1,0:T(8,128)(2,1)}, bf16[8,32,6016]{2,1,0:T(8,128)(2,1)S(1)}, u32[]{:S(2)}, u32[]{:S(2)}) %collective-permute-start) | collective-permute-done | bytes 3080224 | tf_op jit(solution)/shard_map/ppermute | solution.py:204
  47.4 1.2 %shard_map.31 = (f32[128,256]{1,0:T(8,128)S(1)}, f32[136,768]{1,0:T(8,128)S(1)}) custom-call(f32[1,6016]{1,0:T(1,128)S(1)} %reshape.12.coulomb, bf16[256,6016]{1,0:T(8,128)(2,1)S(1)} %bitcast.3, bf16[512,6016]{1,0:T(8,128)(2,1)S(1)} %get-tuple-element.15.left, f32[128,512]{1,0:T(8,128)S(1)} %get-tuple-element.22.give), custom_call_target="tpu_custom_call" | custom-call | tf_op jit(solution)/shard_map/pallas_call | solution.py:158
  48.6 8.4 %collective-permute-start.5 = (f16[136,768]{1,0:T(8,128)(2,1)S(1)}, f16[136,768]{1,0:T(8,128)(2,1)S(1)}, u32[]{:S(2)}, u32[]{:S(2)}) collective-permute-start(f16[136,768]{1,0:T(8,128)(2,1)S(1)} %convert_element_type.30), channel_id=1, source_target_pairs={{0,1},{1,0},{2,3},{3,2},{4,5},{5,4},{6,7},{7,6},{8,9},{9,8},{10,11... | collective-permute-start | bytes 626696 | tf_op jit(solution)/shard_map/ppermute | solution.py:188
  57.0 1.2 %shard_map.29 = (f32[128,256]{1,0:T(8,128)S(1)}, f32[128,128]{1,0:T(8,128)S(1)}, f32[136,384]{1,0:T(8,128)S(1)}) custom-call(f32[1,6016]{1,0:T(1,128)S(1)} %reshape.12.coulomb, bf16[256,6016]{1,0:T(8,128)(2,1)S(1)} %bitcast.4, bf16[512,6016]{1,0:T(8,128)(2,1)S(1)} %get-tuple-element.15.left), custom_call_target="tpu_custom_call" | custom-call | tf_op jit(solution)/shard_map/pallas_call | solution.py:158
  58.2 1.9 %collective-permute-start.2 = (f16[136,384]{1,0:T(8,128)(2,1)S(1)}, f16[136,384]{1,0:T(8,128)(2,1)S(1)}, u32[]{:S(2)}, u32[]{:S(2)}) collective-permute-start(f16[136,384]{1,0:T(8,128)(2,1)S(1)} %convert_element_type.24), channel_id=1, source_target_pairs={{0,1},{1,0},{2,3},{3,2},{4,5},{5,4},{6,7},{7,6},{8,9},{9,8},{10,11... | collective-permute-start | bytes 313352 | tf_op jit(solution)/shard_map/ppermute | solution.py:188
  60.1 11.7 %collective-permute-done.2 = f16[136,384]{1,0:T(8,128)(2,1)S(1)} collective-permute-done((f16[136,384]{1,0:T(8,128)(2,1)S(1)}, f16[136,384]{1,0:T(8,128)(2,1)S(1)}, u32[]{:S(2)}, u32[]{:S(2)}) %collective-permute-start.2) | collective-permute-done | bytes 104480 | tf_op jit(solution)/shard_map/ppermute | solution.py:188
  71.8 0.1 shard_map.30
  72.0 1.9 %collective-permute-start.3 = (f16[136,256]{1,0:T(8,128)(2,1)S(1)}, f16[136,256]{1,0:T(8,128)(2,1)S(1)}, u32[]{:S(2)}, u32[]{:S(2)}) collective-permute-start(f16[136,256]{1,0:T(8,128)(2,1)S(1)} %convert_element_type.26), channel_id=1, source_target_pairs={{0,2},{2,0},{4,6},{6,4},{8,10},{10,8},{12,14},{14,12},{16,18},{18,... | collective-permute-start | bytes 208904 | tf_op jit(solution)/shard_map/ppermute | solution.py:188
  73.9 5.3 %collective-permute-start.4 = (f16[136,256]{1,0:T(8,128)(2,1)S(1)}, f16[136,256]{1,0:T(8,128)(2,1)S(1)}, u32[]{:S(2)}, u32[]{:S(2)}) collective-permute-start(f16[136,256]{1,0:T(8,128)(2,1)S(1)} %convert_element_type.28), channel_id=1, source_target_pairs={{0,510},{2,4},{4,2},{6,8},{8,6},{10,12},{12,10},{14,16},{16,14},{1... | collective-permute-start | bytes 208904 | tf_op jit(solution)/shard_map/ppermute | solution.py:188
  79.3 0.0 collective-permute-done.3
  79.3 5.1 %collective-permute-done.4 = f16[136,256]{1,0:T(8,128)(2,1)S(1)} collective-permute-done((f16[136,256]{1,0:T(8,128)(2,1)S(1)}, f16[136,256]{1,0:T(8,128)(2,1)S(1)}, u32[]{:S(2)}, u32[]{:S(2)}) %collective-permute-start.4) | collective-permute-done | bytes 69664 | tf_op jit(solution)/shard_map/ppermute | solution.py:188
  84.4 0.0 collective-permute-done.5
  84.4 0.8 shard_map.32.filled
  85.3 0.7 shard_map.33
  (8 shorter events, 0.1 us)
Async XLA Ops:
  0.0 13.7 %collective-permute-start.1 = (bf16[8,32,6016]{2,1,0:T(8,128)(2,1)}, bf16[8,32,6016]{2,1,0:T(8,128)(2,1)S(1)}, u32[]{:S(2)}, u32[]{:S(2)}) collective-permute-start(bf16[8,32,6016]{2,1,0:T(8,128)(2,1)} %param.2), channel_id=1, source_target_pairs={{0,2},{2,0},{4,6},{6,4},{8,10},{10,8},{12,14},{14,12},{16,18},{18,... | collective-permute-start | bytes 9240584 | tf_op jit(solution)/shard_map/ppermute | solution.py:205
  1.9 45.4 %collective-permute-start = (bf16[8,32,6016]{2,1,0:T(8,128)(2,1)}, bf16[8,32,6016]{2,1,0:T(8,128)(2,1)S(1)}, u32[]{:S(2)}, u32[]{:S(2)}) collective-permute-start(bf16[8,32,6016]{2,1,0:T(8,128)(2,1)} %param.2), channel_id=1, source_target_pairs={{0,510},{2,4},{4,2},{6,8},{8,6},{10,12},{12,10},{14,16},{16,14},{1... | collective-permute-start | bytes 9240584 | tf_op jit(solution)/shard_map/ppermute | solution.py:204
  13.7 1.9 %copy-start = (bf16[8,32,6016]{2,1,0:T(8,128)(2,1)S(1)}, bf16[8,32,6016]{2,1,0:T(8,128)(2,1)}, u32[]{:S(2)}) copy-start(bf16[8,32,6016]{2,1,0:T(8,128)(2,1)} %param.2) | copy-start | bytes 9240580
  48.6 35.8 %collective-permute-start.5 = (f16[136,768]{1,0:T(8,128)(2,1)S(1)}, f16[136,768]{1,0:T(8,128)(2,1)S(1)}, u32[]{:S(2)}, u32[]{:S(2)}) collective-permute-start(f16[136,768]{1,0:T(8,128)(2,1)S(1)} %convert_element_type.30), channel_id=1, source_target_pairs={{0,1},{1,0},{2,3},{3,2},{4,5},{5,4},{6,7},{7,6},{8,9},{9,8},{10,11... | collective-permute-start | bytes 626696 | tf_op jit(solution)/shard_map/ppermute | solution.py:188
  58.2 13.6 %collective-permute-start.2 = (f16[136,384]{1,0:T(8,128)(2,1)S(1)}, f16[136,384]{1,0:T(8,128)(2,1)S(1)}, u32[]{:S(2)}, u32[]{:S(2)}) collective-permute-start(f16[136,384]{1,0:T(8,128)(2,1)S(1)} %convert_element_type.24), channel_id=1, source_target_pairs={{0,1},{1,0},{2,3},{3,2},{4,5},{5,4},{6,7},{7,6},{8,9},{9,8},{10,11... | collective-permute-start | bytes 313352 | tf_op jit(solution)/shard_map/ppermute | solution.py:188
  72.0 7.3 %collective-permute-start.3 = (f16[136,256]{1,0:T(8,128)(2,1)S(1)}, f16[136,256]{1,0:T(8,128)(2,1)S(1)}, u32[]{:S(2)}, u32[]{:S(2)}) collective-permute-start(f16[136,256]{1,0:T(8,128)(2,1)S(1)} %convert_element_type.26), channel_id=1, source_target_pairs={{0,2},{2,0},{4,6},{6,4},{8,10},{10,8},{12,14},{14,12},{16,18},{18,... | collective-permute-start | bytes 208904 | tf_op jit(solution)/shard_map/ppermute | solution.py:188
  73.9 10.4 %collective-permute-start.4 = (f16[136,256]{1,0:T(8,128)(2,1)S(1)}, f16[136,256]{1,0:T(8,128)(2,1)S(1)}, u32[]{:S(2)}, u32[]{:S(2)}) collective-permute-start(f16[136,256]{1,0:T(8,128)(2,1)S(1)} %convert_element_type.28), channel_id=1, source_target_pairs={{0,510},{2,4},{4,2},{6,8},{8,6},{10,12},{12,10},{14,16},{16,14},{1... | collective-permute-start | bytes 208904 | tf_op jit(solution)/shard_map/ppermute | solution.py:188
